TPU v7x, 128 devices: a whole 4x4x4 slice. The times are simulated.
128 devices in a mesh: prow: 4 (over y_hi, core), pcol: 32 (over x, y_lo, z).
Axes of the slice: x: 4, y: 4 (y_hi: 2, y_lo: 2; y = y_hi * 2 + y_lo), z: 4, core: 2. Of those that a mesh axis runs over, the one named last changes fastest.
Arguments:
- vectors: bfloat16 [2048, 120064], P('pcol', 'prow'), may hold values from -6 to 6
- reflectors: bfloat16 [2, 256, 120064], P(None, 'pcol', 'prow'), may hold values from -6 to 6
- panel_factor: float32 [2, 256, 256], replicated, as said below
Outputs:
- band_vectors: bfloat16 [32, 64, 120064], P('pcol', 'prow')
Inputs may be any that keep to these rules, and one draw needn't show every extreme that they name: `panel_factor`: upper triangular: zero below the diagonal; diagonal entries between 1 / 120064 and 3 / 120064.
All inputs are finite; a program needn't handle non-finite values.
Results may differ from a plain program's by a relative error of at most 0.0095.
Values may be sent and summed in bfloat16 or wider, within the bound.
A program may use at most 192 MiB of HBM per device.

v0:
```python
import jax
import jax.numpy as jnp
from jax import lax
from jax.sharding import PartitionSpec as P


def over_pieces(value, axis):
    return lax.all_gather(value, axis).astype(jnp.float32).sum(0)


def finish_panel(current, panel, factor, projected):
    scaled = lax.dot_general(
        projected,
        factor,
        (((1,), (1,)), ((), ())),
        precision=lax.Precision.HIGHEST,
        preferred_element_type=jnp.float32,
    ).astype(jnp.bfloat16)
    updated = current.astype(jnp.float32) - jnp.dot(
        scaled, panel, preferred_element_type=jnp.float32
    )
    return updated.astype(jnp.bfloat16)


def partial_products(current, panel):
    return lax.dot_general(
        current, panel, (((1,), (1,)), ((), ())), preferred_element_type=jnp.float32
    )


def apply_panel(current, panel, factor):
    partial_sum = partial_products(current, panel)
    projected = over_pieces(partial_sum.astype(jnp.bfloat16), "prow").astype(jnp.float32)
    return finish_panel(current, panel, factor, projected)


def body(vectors, reflectors, panel_factor):
    current = vectors
    for number in range(reflectors.shape[0]):
        single = lax.all_gather(reflectors[number], "pcol", axis=0, tiled=True)
        current = apply_panel(current, single, panel_factor[number])
    owned_rows = lax.all_to_all(current, "prow", split_axis=0, concat_axis=1, tiled=True)
    return owned_rows[None]


def solution(mesh):
    placed = (P("pcol", "prow"), P(None, "pcol", "prow"), P())
    return jax.shard_map(
        body, mesh=mesh, in_specs=placed, out_specs=P("pcol", "prow", None), check_vma=False
    )
```

profile of v0, /device:TPU:1, one launch (start us, length us, event | category | flops | bytes accessed | tf_op | source)
XLA Modules:
  0.0 474.5 jit_solution(8055613551530028033)
XLA Ops:
  6.5 0.0 all-gather.7.cloned.1.call-start
  6.5 2.2 fusion.18
  8.7 0.0 all-gather.7.cloned.1.call-update
  8.8 0.0 all-gather.9.cloned.1.call-start
  8.8 0.7 all-gather.9.cloned.1.call-update
  9.5 0.0 copy-start
  9.5 172.4 %all-gather.7.cloned.1.call-done = bf16[1,256,30016]{2,1,0:T(8,128)(2,1)} async-done(((bf16[1,8,30016]{2,1,0:T(8,128)(2,1)}), bf16[1,256,30016]{2,1,0:T(8,128)(2,1)}) %all-gather.7.cloned.1.call-update) | async-done | bytes 15368208 | tf_op jit(solution)/shard_map/all_gather | solution.py:40
  181.9 11.2 %fusion.8 = bf16[64,256]{1,0:T(8,128)(2,1)S(1)} fusion(bf16[64,30016]{1,0:T(8,128)(2,1)} %param.3, bf16[1,256,30016]{2,1,0:T(8,128)(2,1)} %all-gather.7.cloned.1.call-done), kind=kOutput, calls=%fused_computation.10 | convolution fusion | flops 983580672 | bytes 19243008 | tf_op jit(solution)/shard_map/dot_general | solution.py:26
  193.1 23.4 %all-gather.1 = bf16[256,256]{1,0:T(8,128)(2,1)S(1)} all-gather(bf16[64,256]{1,0:T(8,128)(2,1)S(1)} %fusion.8), channel_id=3, replica_groups=mesh['prow'=4,'pcol'=32] {'prow'}, dimensions={0}, use_global_device_ids=true | all-gather | bytes 163840 | tf_op jit(solution)/shard_map/all_gather | solution.py:8
  216.6 0.0 copy-done
  216.6 0.4 convolution_convert_fusion.1
  216.9 10.7 %fusion = bf16[64,30016]{1,0:T(8,128)(2,1)} fusion(bf16[64,256]{1,0:T(8,128)(2,1)S(1)} %convolution_convert_fusion.1, bf16[1,256,30016]{2,1,0:T(8,128)(2,1)} %all-gather.7.cloned.1.call-done, bf16[64,30016]{1,0:T(8,128)(2,1)} %param.3), kind=kOutput, calls=%fused_computation.2 | convolution fusion | flops 989327360 | bytes 23085056 | tf_op jit(solution)/shard_map/dot_general | solution.py:19
  227.7 138.5 %all-gather.9.cloned.1.call-done = bf16[1,256,30016]{2,1,0:T(8,128)(2,1)} async-done(((bf16[1,8,30016]{2,1,0:T(8,128)(2,1)}), bf16[1,256,30016]{2,1,0:T(8,128)(2,1)}) %all-gather.9.cloned.1.call-update) | async-done | bytes 15368208 | tf_op jit(solution)/shard_map/all_gather | solution.py:40
  366.2 11.2 %fusion.11 = bf16[64,256]{1,0:T(8,128)(2,1)S(1)} fusion(bf16[64,30016]{1,0:T(8,128)(2,1)} %fusion, bf16[1,256,30016]{2,1,0:T(8,128)(2,1)} %all-gather.9.cloned.1.call-done), kind=kOutput, calls=%fused_computation.11 | convolution fusion | flops 983580672 | bytes 19243008 | tf_op jit(solution)/shard_map/dot_general | solution.py:26
  377.4 22.6 %all-gather.3 = bf16[256,256]{1,0:T(8,128)(2,1)S(1)} all-gather(bf16[64,256]{1,0:T(8,128)(2,1)S(1)} %fusion.11), channel_id=5, replica_groups=mesh['prow'=4,'pcol'=32] {'prow'}, dimensions={0}, use_global_device_ids=true | all-gather | bytes 163840 | tf_op jit(solution)/shard_map/all_gather | solution.py:8
  400.1 0.4 convolution_convert_fusion
  400.4 8.7 %fusion.1 = bf16[64,30016]{1,0:T(8,128)(2,1)S(1)} fusion(bf16[64,256]{1,0:T(8,128)(2,1)S(1)} %convolution_convert_fusion, bf16[1,256,30016]{2,1,0:T(8,128)(2,1)} %all-gather.9.cloned.1.call-done, bf16[64,30016]{1,0:T(8,128)(2,1)} %fusion), kind=kOutput, calls=%fused_computation.3 | convolution fusion | flops 989327360 | bytes 23085056 | tf_op jit(solution)/shard_map/dot_general | solution.py:19
  409.1 49.0 %all_to_all.16 = bf16[4,16,30016]{2,1,0:T(8,128)(2,1)S(1)} all-to-all(bf16[4,16,30016]{2,1,0:T(8,128)(2,1)S(1)} %bitcast.32), channel_id=1, replica_groups=mesh['prow'=4,'pcol'=32] {'prow'}, dimensions={0} | all-to-all | bytes 7684096 | tf_op jit(solution)/shard_map/all_to_all | solution.py:42
  458.1 3.3 copy.4
  461.5 6.2 %broadcast_in_dim.3 = bf16[1,16,120064]{2,1,0:T(8,128)(2,1)} reshape(bf16[16,4,30016]{2,1,0:T(4,128)(2,1)} %copy.4) | data formatting | bytes 7684096 | tf_op jit(solution)/shard_map/broadcast_in_dim | solution.py:43
  (2 shorter events, 0.0 us)
Async XLA Ops:
  6.5 175.3 %all-gather.7.cloned.1.call-start = ((), (), s32[]{:S(2)}) async-start(), calls=%async_computation.1 | async-start | bytes 15882240 | tf_op jit(solution)/shard_map/all_gather | solution.py:40
  8.8 357.4 %all-gather.9.cloned.1.call-start = ((), (), s32[]{:S(2)}) async-start(), calls=%async_computation.2 | async-start | bytes 15882240 | tf_op jit(solution)/shard_map/all_gather | solution.py:40
  9.5 207.1 %copy-start = (f32[2,256,256]{2,1,0:T(8,128)S(1)}, f32[2,256,256]{2,1,0:T(8,128)}, u32[]{:S(2)}) copy-start(f32[2,256,256]{2,1,0:T(8,128)} %param.5) | copy-start | bytes 1572868
Sparse Core Ops, SparseCore 0:
  9.0 172.8 all-gather.6
  183.5 182.6 all-gather.8
where the time goes:
time: 475 us; the launch traced here: 474 us
  waiting for transfers between devices  312 us (66%)
  blocking collectives  95 us (20%)
  matrix products  42.6 us (9%)
  between operations  13.4 us (3%)
  local copies, waits for them, and re-layouts  11.7 us (2%)
    all_gather x2, waiting for transfers between devices, body(): single = lax.all_gather(reflectors[number], 'pcol', axis=0, tiled=True)  311 us
    all_to_all x1, blocking collectives, body(): lax.all_to_all(current, 'prow', split_axis=0, concat_axis=1, tiled=True)  49 us
    all_gather x2, blocking collectives, over_pieces(): return lax.all_gather(value, axis).astype(jnp.float32).sum(0)  46 us
    dot_general x2, matrix products, partial_products(): lax.dot_general(current, panel, (((1,), (1,)), ((), ())), preferred_eleme...  22.5 us
    dot_general x2, matrix products, finish_panel(): jnp.dot(scaled, panel, preferred_element_type=jnp.float32)  19.4 us
  transfers between devices with their start and end apart: 2, of which 2 were waited for; matrix products, arithmetic and copies ran while one was open for 5% of the time, Pallas kernels for 0%

commit v1 on v0

v1 whole, which is shorter than its diff:
```python
import functools

import jax
import jax.numpy as jnp
from jax import lax
from jax.experimental import pallas as pl
from jax.experimental.pallas import tpu as pltpu
from jax.sharding import PartitionSpec as P

X, YL, Z, R = 4, 2, 4, 4
Q = YL * Z
GROUP = Q * R
BF16, F32 = jnp.bfloat16, jnp.float32


def kernel(
    dims,
    v_hbm, r_hbm, v_tail, r_tail, factor,
    out,
    v_loc, r_loc, v_all, r_all, p_send, p_recv, g_send, g_recv, g_own, g_all, s_own, s_all,
    ld_sem, own_sem, r_ssem, r_rsem, x_ssem, v_ssem, v_rsem,
    gs_ssem, gs_rsem, ga_ssem, ga_rsem, ps_ssem, ps_rsem, sa_ssem, sa_rsem, o_ssem, o_rsem, o_own,
):
    rows, panel, whole, valid, chunk, step = dims
    per = rows // R
    share = panel // (X * Q)
    prow, pcol = lax.axis_index("prow"), lax.axis_index("pcol")
    x, yl, z = pcol // Q, lax.rem(pcol // Z, YL), lax.rem(pcol, Z)
    h, k = prow // 2, lax.rem(prow, 2)

    def place(dx, dy, dz, dr):
        far = lax.rem(x + dx, X) * Q + lax.rem(yl + dy, YL) * Z + lax.rem(z + dz, Z)
        across = lax.rem(h + dr // 2, 2) * 2 + lax.rem(k + dr % 2, 2)
        return across, far

    def place_of(d):
        dy, dz, dr = d // 16, lax.rem(d // 4, 4), lax.rem(d, 4)
        far = x * Q + lax.rem(yl + dy, YL) * Z + lax.rem(z + dz, Z)
        across = lax.rem(h + dr // 2, 2) * 2 + lax.rem(k + lax.rem(dr, 2), 2)
        return across, far

    def mirror(d):
        dy, dz, dr = d // 16, lax.rem(d // 4, 4), lax.rem(d, 4)
        return dy * 16 + lax.rem(4 - dz, 4) * 4 + dr

    def send(src, dst, ssem, rsem, to):
        return pltpu.make_async_remote_copy(
            src_ref=src, dst_ref=dst, send_sem=ssem, recv_sem=rsem,
            device_id=to, device_id_type=pl.DeviceIdType.MESH,
        )

    def arrived(ref, sem):
        pltpu.make_async_copy(ref, ref, sem).wait()

    load_r = pltpu.make_async_copy(r_hbm.at[:, :, pl.ds(0, whole)], r_loc.at[:, :, pl.ds(0, whole)], ld_sem.at[0])
    load_v = pltpu.make_async_copy(v_hbm.at[:, pl.ds(0, whole)], v_loc.at[:, pl.ds(0, whole)], ld_sem.at[1])
    load_r.start()
    load_v.start()

    barrier = pltpu.get_barrier_semaphore()

    @pl.loop(1, GROUP)
    def _(d):
        pl.semaphore_signal(barrier, inc=1, device_id=place_of(d), device_id_type=pl.DeviceIdType.MESH)

    for dx in range(1, X):
        pl.semaphore_signal(barrier, inc=1, device_id=place(dx, 0, 0, 0), device_id_type=pl.DeviceIdType.MESH)

    edge = v_loc.shape[1] - whole
    lane = lax.broadcasted_iota(jnp.int32, (rows, 128), 1)
    v_loc[:, whole:] = jnp.zeros((rows, edge), BF16)
    v_loc[:, whole:whole + 128] = jnp.where(lane < valid, v_tail[...].astype(F32), 0.0).astype(BF16)
    lane8 = lax.broadcasted_iota(jnp.int32, (share, 128), 1)
    for p in range(2):
        r_loc[p, :, whole:] = jnp.zeros((share, edge), BF16)
        r_loc[p, :, whole:whole + 128] = jnp.where(lane8 < valid, r_tail[p].astype(F32), 0.0).astype(BF16)

    pl.semaphore_wait(barrier, GROUP - 1 + X - 1)

    offsets = [(dy, dz) for dz in (1, 3, 2, 0) for dy in (0, 1) if (dy, dz) != (0, 0)]
    mine = pl.ds(pl.multiple_of(pcol * share, share), share)

    def columns(dy, dz):
        q = lax.rem(yl + dy, YL) * Z + lax.rem(z + dz, Z)
        return pl.ds(pl.multiple_of(q * chunk, 128), chunk)

    load_r.wait()
    r_out = []
    for dy, dz in offsets:
        back = dy * 4 + (4 - dz) % 4
        copy = send(r_loc.at[:, :, columns(dy, dz)], r_all.at[:, mine, :], r_ssem.at[dy * 4 + dz],
                    r_rsem.at[back], place(0, dy, dz, 0))
        copy.start()
        r_out.append(copy)
    own_r = pltpu.make_async_copy(r_loc.at[:, :, columns(0, 0)], r_all.at[:, mine, :], own_sem.at[0])
    own_r.start()
    load_v.wait()
    v_out = []
    for dy, dz in offsets:
        back = dy * 4 + (4 - dz) % 4
        copy = send(v_loc.at[:, columns(dy, dz)], v_all.at[pl.ds(rows * back, rows), :], v_ssem.at[dy * 4 + dz],
                    v_rsem.at[back], place(0, dy, dz, 0))
        copy.start()
        v_out.append(copy)
    own_v = pltpu.make_async_copy(v_loc.at[:, columns(0, 0)], v_all.at[pl.ds(0, rows), :], own_sem.at[1])
    own_v.start()

    def held(dx, dy, dz):
        source = place(dx, dy, dz, 0)[1]
        return r_all.at[:, pl.ds(pl.multiple_of(source * share, share), share), :]

    x_out = []
    for dy, dz in [(0, 0)] + [(dy, (4 - dz) % 4) for dy, dz in offsets]:
        slot = dy * 4 + dz
        piece = held(0, dy, dz)
        if slot == 0:
            own_r.wait()
        else:
            arrived(piece, r_rsem.at[slot])
        for dx in (1, 3, 2):
            at = (4 - dx) * Q + slot
            copy = send(piece, piece, x_ssem.at[dx * Q + slot], r_rsem.at[at], place(dx, 0, 0, 0))
            copy.start()
            x_out.append(copy)
    for dx in (1, 3, 2):
        for dy, dz in [(0, 0)] + [(dy, (4 - dz) % 4) for dy, dz in offsets]:
            arrived(held(dx, dy, dz), r_rsem.at[dx * Q + dy * 4 + dz])

    nt = (((1,), (1,)), ((), ()))

    g_send[...] = jnp.zeros_like(g_send)

    @pl.loop(0, chunk // step)
    def _(j):
        cols = pl.ds(pl.multiple_of(j * step, 128), step)
        g_send[...] += lax.dot_general(r_all[0, :, cols], r_all[1, :, cols], nt, preferred_element_type=F32)

    def order_of(d):
        across, far = place_of(d)
        return lax.rem(far, Q) * R + across

    def own_rows(d, count):
        return pl.ds(pl.multiple_of(order_of(d) * count, count), count)

    part = panel // GROUP

    def g_out(d):
        return send(g_send.at[own_rows(d, part), :], g_recv.at[mirror(d)], gs_ssem.at[d], gs_rsem.at[mirror(d)], place_of(d))

    @pl.loop(1, GROUP)
    def _(d):
        g_out(d).start()

    def block(dy, dz):
        slot = dy * 4 + dz
        for p in range(2):
            def body(j, total):
                cols = pl.ds(pl.multiple_of(j * step, 128), step)
                return total + lax.dot_general(
                    v_all[pl.ds(slot * rows, rows), cols], r_all[p, :, cols], nt, preferred_element_type=F32)
            total = lax.fori_loop(0, chunk // step, body, jnp.zeros((rows, panel), F32))
            p_send[pl.ds(slot * rows, rows), p * panel:(p + 1) * panel] = total.astype(BF16)

    def block_rows(d):
        across, _ = place_of(d)
        return pl.ds(pl.multiple_of((d // R) * rows + across * per, per), per)

    def p_out(d):
        return send(p_send.at[block_rows(d), :], p_recv.at[mirror(d)], ps_ssem.at[d], ps_rsem.at[mirror(d)], place_of(d))

    def p_start(dy, dz):
        slot = dy * 4 + dz
        for dr in range(R):
            if slot * R + dr:
                p_out(slot * R + dr).start()

    own_v.wait()
    block(0, 0)
    p_start(0, 0)

    def g_finish():
        @pl.loop(1, GROUP)
        def _(d):
            arrived(g_recv.at[d], gs_rsem.at[d])
        g_own[...] = jnp.sum(g_recv[1:], axis=0) + g_send[own_rows(0, part), :]

        @pl.loop(1, GROUP)
        def _(d):
            send(g_own, g_all.at[own_rows(0, part), :], ga_ssem.at[d], ga_rsem.at[mirror(d)], place_of(d)).start()
        g_all[own_rows(0, part), :] = g_own[...]

    for number, (dy, dz) in enumerate([(dy, (4 - dz) % 4) for dy, dz in offsets]):
        slot = dy * 4 + dz
        arrived(v_all.at[pl.ds(slot * rows, rows), :], v_rsem.at[slot])
        block(dy, dz)
        p_start(dy, dz)
        if number == 3:
            g_finish()

    @pl.loop(1, GROUP)
    def _(d):
        arrived(p_recv.at[d], ps_rsem.at[d])

    product = p_send[block_rows(0), :].astype(F32)
    product = product + jnp.sum(p_recv[1:].astype(F32), axis=0)

    def exact(a, b, dims):
        return lax.dot_general(a, b, dims, precision=lax.Precision.HIGHEST, preferred_element_type=F32)

    first = exact(product[:, :panel], factor[0], nt).astype(BF16)

    @pl.loop(1, GROUP)
    def _(d):
        arrived(g_all.at[own_rows(d, part), :], ga_rsem.at[d])
    rest = product[:, panel:] - exact(first.astype(F32), g_all[...], (((1,), (0,)), ((), ())))
    second = exact(rest, factor[1], nt).astype(BF16)
    s_own[:, :panel] = first
    s_own[:, panel:] = second

    def s_slot(d, across):
        return pl.ds(pl.multiple_of((d // R) * rows + across * per, per), per)

    def s_out(d):
        return send(s_own, s_all.at[s_slot(mirror(d), prow), :], sa_ssem.at[d], sa_rsem.at[mirror(d)], place_of(d))

    @pl.loop(1, GROUP)
    def _(d):
        s_out(d).start()
    s_all[s_slot(0, prow), :] = s_own[...]

    @pl.loop(1, GROUP)
    def _(d):
        arrived(s_all.at[s_slot(d, place_of(d)[0]), :], sa_rsem.at[d])

    base = lax.rem(pcol, Q) * chunk

    def put(d, j):
        there = pl.ds(pl.multiple_of(base + j * step, 128), step)
        here = pl.ds(pl.multiple_of(j * step, 128), step)
        return send(v_all.at[block_rows(d), here], out.at[prow, :, there], o_ssem.at[d], o_rsem.at[mirror(d)], place_of(d))

    def keep(j):
        there = pl.ds(pl.multiple_of(base + j * step, 128), step)
        here = pl.ds(pl.multiple_of(j * step, 128), step)
        return pltpu.make_async_copy(v_all.at[block_rows(0), here], out.at[prow, :, there], o_own.at[0])

    @pl.loop(0, chunk // step)
    def _(j):
        cols = pl.ds(pl.multiple_of(j * step, 128), step)
        change = jnp.dot(s_all[:, :panel], r_all[0, :, cols], preferred_element_type=F32)
        change = change + jnp.dot(s_all[:, panel:], r_all[1, :, cols], preferred_element_type=F32)
        v_all[:, cols] = (v_all[:, cols].astype(F32) - change).astype(BF16)

        @pl.loop(1, GROUP)
        def _(d):
            put(d, j).start()
        keep(j).start()

    for copy in r_out + v_out + x_out:
        copy.wait_send()
    whole_rows = out.at[0, :, pl.ds(0, chunk)]
    arrived(whole_rows, o_own.at[0])

    @pl.loop(1, GROUP)
    def _(d):
        arrived(g_recv.at[0], gs_ssem.at[d])
        arrived(g_own, ga_ssem.at[d])
        arrived(p_recv.at[0], ps_ssem.at[d])
        arrived(s_own, sa_ssem.at[d])
        arrived(whole_rows, o_ssem.at[d])
        across, far = place_of(d)
        there = pl.ds(pl.multiple_of(lax.rem(far, Q) * chunk, 128), chunk)
        arrived(out.at[across, :, there], o_rsem.at[d])


def body(vectors, reflectors, panel_factor):
    rows, width = vectors.shape
    panel = panel_factor.shape[1]
    share = reflectors.shape[1]
    tiles = pl.cdiv(width, 128)
    chunk = pl.cdiv(tiles, Q) * 128
    whole = (tiles - 1) * 128
    step = chunk // 6
    dims = (rows, panel, whole, width - whole, chunk, step)
    per = rows // R
    any_spec = pl.BlockSpec(memory_space=pl.ANY)
    dma = pltpu.SemaphoreType.DMA
    gathered = pl.pallas_call(
        functools.partial(kernel, dims),
        grid=(1,),
        out_shape=jax.ShapeDtypeStruct((R, per, chunk * Q), BF16),
        in_specs=[
            any_spec, any_spec,
            pl.BlockSpec((rows, 128), lambda i: (0, tiles - 1)),
            pl.BlockSpec((2, share, 128), lambda i: (0, 0, tiles - 1)),
            pl.BlockSpec((2, panel, panel), lambda i: (0, 0, 0)),
        ],
        out_specs=any_spec,
        scratch_shapes=[
            pltpu.VMEM((rows, chunk * Q), BF16),
            pltpu.VMEM((2, share, chunk * Q), BF16),
            pltpu.VMEM((rows * Q, chunk), BF16),
            pltpu.VMEM((2, panel, chunk), BF16),
            pltpu.VMEM((rows * Q, 2 * panel), BF16),
            pltpu.VMEM((GROUP, per, 2 * panel), BF16),
            pltpu.VMEM((panel, panel), F32),
            pltpu.VMEM((GROUP, panel // GROUP, panel), F32),
            pltpu.VMEM((panel // GROUP, panel), F32),
            pltpu.VMEM((panel, panel), F32),
            pltpu.VMEM((per, 2 * panel), BF16),
            pltpu.VMEM((rows * Q, 2 * panel), BF16),
            dma((2,)), dma((2,)), dma((Q,)), dma((X * Q,)), dma((X * Q,)), dma((Q,)), dma((Q,)),
            dma((GROUP,)), dma((GROUP,)), dma((GROUP,)), dma((GROUP,)), dma((GROUP,)), dma((GROUP,)),
            dma((GROUP,)), dma((GROUP,)), dma((GROUP,)), dma((GROUP,)), dma((1,)),
        ],
        compiler_params=pltpu.CompilerParams(
            collective_id=0, has_side_effects=True, vmem_limit_bytes=48 * 1024 * 1024
        ),
        name="back_transform",
    )(vectors, reflectors, vectors, reflectors, panel_factor)
    return jnp.concatenate([gathered[r, :, :width] for r in range(R)], axis=1)[None]


def solution(mesh):
    placed = (P("pcol", "prow"), P(None, "pcol", "prow"), P())
    return jax.shard_map(
        body, mesh=mesh, in_specs=placed, out_specs=P("pcol", "prow", None), check_vma=False
    )
```

time: 475 us -> 183 us (0.39)
  waiting for transfers between devices: 312 us -> 0 us
  Pallas kernels: 0 us -> 151 us
  blocking collectives: 95 us -> 0 us
  matrix products: 42.6 us -> 0 us
  local copies, waits for them, and re-layouts: 11.7 us -> 31.3 us
  between operations: 13.4 us -> 0.01 us
    all_gather x2 -> x0, waiting for transfers between devices: 311 us -> none  [body(): single = lax.all_gather(reflectors[number], 'pcol', axis=0, tiled=True)]
    pallas_call x0 -> x1, Pallas kernels: none -> 151 us  [body(): pl.pallas_call(functools.partial(kernel, dims), grid=(1,), out_shape=jax....]
    all_to_all x1 -> x0, blocking collectives: 49 us -> none  [body(): lax.all_to_all(current, 'prow', split_axis=0, concat_axis=1, tiled=True)]
    all_gather x2 -> x0, blocking collectives: 46 us -> none  [over_pieces(): return lax.all_gather(value, axis).astype(jnp.float32).sum(0)]
    dot_general x6 -> x0, matrix products: 42.6 us -> none  [the longest x2 22.5 us: partial_products(): lax.dot_general(current, panel, (((1,), (1,)), ((), ())), preferred_eleme...]
    unnamed x2 -> x9, local copies, waits for them, and re-layouts: 0.01 us -> 21.9 us
    broadcast_in_dim x1 -> x0, local copies, waits for them, and re-layouts: 6.17 us -> none  [body(): return owned_rows[None]]
    concatenate x0 -> x1, local copies, waits for them, and re-layouts: none -> 6.1 us  [body(): jnp.concatenate([gathered[r, :, :width] for r in range(R)], axis=1)[None]]
  transfers between devices with their start and end apart: 2 -> 0, of which waited for: 2 -> 0; matrix products, arithmetic and copies ran while one was open for 5% -> 0% of each run, Pallas kernels for 0% -> 0%
where the time goes in v1:
time: 183 us; the launch traced here: 182 us
  Pallas kernels  151 us (83%)
  local copies, waits for them, and re-layouts  31.3 us (17%)
    pallas_call x1, Pallas kernels, body(): pl.pallas_call(functools.partial(kernel, dims), grid=(1,), out_shape=jax....  151 us
    unnamed x9, local copies, waits for them, and re-layouts  21.9 us
    concatenate x1, local copies, waits for them, and re-layouts, body(): jnp.concatenate([gathered[r, :, :width] for r in range(R)], axis=1)[None]  6.1 us

profile of v1, /device:TPU:1, one launch (start us, length us, event | category | flops | bytes accessed | tf_op | source)
XLA Modules:
  0.0 182.1 jit_solution(13951433712514210606)
XLA Ops:
  0.0 0.0 copy-start
  0.0 2.1 %copy-done = bf16[64,30016]{1,0:T(8,128)(2,1)S(1)} copy-done((bf16[64,30016]{1,0:T(8,128)(2,1)S(1)}, bf16[64,30016]{1,0:T(8,128)(2,1)}, u32[]{:S(2)}) %copy-start) | copy-done | bytes 3842072
  2.1 0.0 copy-start.1
  2.1 1.2 copy-done.1
  3.3 0.0 copy-start.2
  3.3 1.0 copy-done.2
  4.3 150.8 %back_transform.1 = bf16[4,16,30720]{2,1,0:T(8,128)(2,1)} custom-call(bf16[64,30016]{1,0:T(8,128)(2,1)S(1)} %copy-done, bf16[2,8,30016]{2,1,0:T(8,128)(2,1)S(1)} %copy-done.1, bf16[64,30016]{1,0:T(8,128)(2,1)S(1)} %copy-done, bf16[2,8,30016]{2,1,0:T(8,128)(2,1)S(1)} %copy-done.1, f32[2,256,256]{2,1,0:T(8,128)S(1)} %copy-done.2), custom_call_target="tpu_custom_call" | custom-call | tf_op jit(solution)/shard_map/back_transform/pallas_call | solution.py:288
  155.2 3.3 %slice_bitcast_fusion = (bf16[16,30016]{1,0:T(8,128)(2,1)S(1)}, bf16[16,30016]{1,0:T(8,128)(2,1)S(1)}, bf16[16,30016]{1,0:T(8,128)(2,1)S(1)}, bf16[16,30016]{1,0:T(8,128)(2,1)}) fusion(bf16[4,16,30720]{2,1,0:T(8,128)(2,1)} %back_transform.1), kind=kLoop, calls=%fused_computation | loop fusion | bytes 7684096 | tf_op jit(solution)/shard_map/squeeze | solution.py:321
  158.4 5.9 %dynamic-update-slice = bf16[16,120064]{1,0:T(8,128)(2,1)} dynamic-update-slice(bf16[16,120064]{1,0:T(8,128)(2,1)} %custom-call, bf16[16,30016]{1,0:T(8,128)(2,1)} %get-tuple-element.8, s32[]{} %constant.1, s32[]{} %constant.1) | dynamic-update-slice | bytes 1921028
  164.3 6.2 %dynamic-update-slice.1 = bf16[16,120064]{1,0:T(8,128)(2,1)} dynamic-update-slice(bf16[16,120064]{1,0:T(8,128)(2,1)} %dynamic-update-slice, bf16[16,30016]{1,0:T(8,128)(2,1)S(1)} %get-tuple-element.7, s32[]{} %constant.1, s32[]{} %constant.2) | dynamic-update-slice | bytes 1921028
  170.5 5.6 %dynamic-update-slice.2 = bf16[16,120064]{1,0:T(8,128)(2,1)} dynamic-update-slice(bf16[16,120064]{1,0:T(8,128)(2,1)} %dynamic-update-slice.1, bf16[16,30016]{1,0:T(8,128)(2,1)S(1)} %get-tuple-element.6, s32[]{} %constant.1, s32[]{} %constant.3) | dynamic-update-slice | bytes 1921028
  176.0 6.1 %dynamic-update-slice.3 = bf16[16,120064]{1,0:T(8,128)(2,1)} dynamic-update-slice(bf16[16,120064]{1,0:T(8,128)(2,1)} %dynamic-update-slice.2, bf16[16,30016]{1,0:T(8,128)(2,1)S(1)} %get-tuple-element.5, s32[]{} %constant.1, s32[]{} %constant.4) | dynamic-update-slice | bytes 1921028 | tf_op jit(solution)/shard_map/concatenate | solution.py:321
  (1 shorter events, 0.0 us)
Async XLA Ops:
  0.0 2.1 %copy-start = (bf16[64,30016]{1,0:T(8,128)(2,1)S(1)}, bf16[64,30016]{1,0:T(8,128)(2,1)}, u32[]{:S(2)}) copy-start(bf16[64,30016]{1,0:T(8,128)(2,1)} %v_tail.1) | copy-start | bytes 11526148
  2.1 1.2 copy-start.1
  3.3 1.0 copy-start.2

commit v2 on v1

--- a/solution.py
+++ b/solution.py
@@ -271,6 +271,37 @@
         across, far = place_of(d)
         there = pl.ds(pl.multiple_of(lax.rem(far, Q) * chunk, 128), chunk)
         arrived(out.at[across, :, there], o_rsem.at[d])
+
+
+def joined(width, pieces, out, held, line, in_sem, out_sem):
+    loads = [pltpu.make_async_copy(pieces.at[r], held.at[r], in_sem.at[r]) for r in range(R)]
+    for load in loads:
+        load.start()
+    stores = []
+    rows = held.shape[1]
+    for r in range(R):
+        loads[r].wait()
+        first, shift = r * width // 128 * 128, r * width % 128
+        end = (r + 1) * width // 128 * 128
+        if shift == 0:
+            source = held.at[r, :, pl.ds(0, end - first)]
+        else:
+            count = (end - first) // 128
+            lane = lax.broadcasted_iota(jnp.int32, (rows, 128), 1)
+            keep = held[r - 1, :, pl.ds(first - (r - 1) * width // 128 * 128, 128)].astype(F32)
+            turned = pltpu.roll(held[r, :, :128].astype(F32), shift, 1)
+            line[r // 2, :, :128] = jnp.where(lane < shift, keep, turned).astype(BF16)
+            width_step = 13 * 128
+            for a in range(128, count * 128, width_step):
+                n = min(width_step, count * 128 - a)
+                wide = held[r, :, a - 128:a + n].astype(F32)
+                line[r // 2, :, a:a + n] = pltpu.roll(wide, shift, 1)[:, 128:].astype(BF16)
+            source = line.at[r // 2]
+        store = pltpu.make_async_copy(source, out.at[:, pl.ds(first, end - first)], out_sem.at[r])
+        store.start()
+        stores.append(store)
+    for store in stores:
+        store.wait()
 
 
 def body(vectors, reflectors, panel_factor):
@@ -314,11 +345,23 @@
             dma((GROUP,)), dma((GROUP,)), dma((GROUP,)), dma((GROUP,)), dma((1,)),
         ],
         compiler_params=pltpu.CompilerParams(
-            collective_id=0, has_side_effects=True, vmem_limit_bytes=48 * 1024 * 1024
+            collective_id=0, has_side_effects=True, vmem_limit_bytes=61 * 1024 * 1024
         ),
         name="back_transform",
     )(vectors, reflectors, vectors, reflectors, panel_factor)
-    return jnp.concatenate([gathered[r, :, :width] for r in range(R)], axis=1)[None]
+    line = R * width // 128 * 128 - 3 * width // 128 * 128
+    rows_out = pl.pallas_call(
+        functools.partial(joined, width),
+        out_shape=jax.ShapeDtypeStruct((per, R * width), BF16),
+        in_specs=[any_spec],
+        out_specs=any_spec,
+        scratch_shapes=[
+            pltpu.VMEM((R, per, chunk * Q), BF16), pltpu.VMEM((2, per, line), BF16), dma((R,)), dma((R,)),
+        ],
+        compiler_params=pltpu.CompilerParams(vmem_limit_bytes=61 * 1024 * 1024),
+        name="joined",
+    )(gathered)
+    return rows_out[None]
 
 
 def solution(mesh):

time: 183 us -> 154 us (0.84)
  local copies, waits for them, and re-layouts: 31.3 us -> 0 us
  Pallas kernels: 151 us -> 154 us
    unnamed x9 -> x0, local copies, waits for them, and re-layouts: 21.9 us -> none
    concatenate x1 -> x0, local copies, waits for them, and re-layouts: 6.1 us -> none  [body(): jnp.concatenate([gathered[r, :, :width] for r in range(R)], axis=1)[None]]
    pallas_call x0 -> x1, Pallas kernels: none -> 3.48 us  [body(): pl.pallas_call(functools.partial(joined, width), out_shape=jax.ShapeDtype...]
    squeeze x1 -> x0, local copies, waits for them, and re-layouts: 3.28 us -> none  [body(): gathered[r, :, :width]]
where the time goes in v2:
time: 154 us
  Pallas kernels  154 us (100%)
    pallas_call x1, Pallas kernels, body(): pl.pallas_call(functools.partial(kernel, dims), grid=(1,), out_shape=jax....  151 us
    pallas_call x1, Pallas kernels, body(): pl.pallas_call(functools.partial(joined, width), out_shape=jax.ShapeDtype...  3.48 us

profile of v2, /device:TPU:1, one launch (start us, length us, event | category | flops | bytes accessed | tf_op | source)
XLA Modules:
  0.0 154.3 jit_solution(7147756656446579947)
XLA Ops:
  0.0 150.9 %back_transform.1.pieces = bf16[4,16,30720]{2,1,0:T(8,128)(2,1)} custom-call(bf16[64,30016]{1,0:T(8,128)(2,1)} %v_tail.1, bf16[2,8,30016]{2,1,0:T(8,128)(2,1)} %r_tail.1, bf16[64,30016]{1,0:T(8,128)(2,1)} %v_tail.1, bf16[2,8,30016]{2,1,0:T(8,128)(2,1)} %r_tail.1, f32[2,256,256]{2,1,0:T(8,128)} %factor.1), custom_call_target="tpu_custom_call" | custom-call | tf_op jit(solution)/shard_map/back_transform/pallas_call | solution.py:319
  150.9 3.5 %joined.1 = bf16[16,120064]{1,0:T(8,128)(2,1)} custom-call(bf16[4,16,30720]{2,1,0:T(8,128)(2,1)} %back_transform.1.pieces), custom_call_target="tpu_custom_call" | custom-call | tf_op jit(solution)/shard_map/joined/pallas_call | solution.py:353

commit v3 on v0

v3 whole, which is shorter than its diff:
```python
import functools

import jax
import jax.numpy as jnp
from jax import lax
from jax.experimental import pallas as pl
from jax.experimental.pallas import tpu as pltpu
from jax.sharding import PartitionSpec as P

X, YL, Z, R = 4, 2, 4, 4
Q = YL * Z
GROUP = Q * R
ORDER = ((0, 0), (0, 3), (0, 1), (1, 3), (1, 1), (0, 2), (1, 2), (1, 0))
SLOT = {pair: number for number, pair in enumerate(ORDER)}
OTHERS = range(1, GROUP)
HELD = 0
BF16, F32 = jnp.bfloat16, jnp.float32
NT = (((1,), (1,)), ((), ()))


def mirror(d):
    dy, dz = ORDER[d // R]
    return SLOT[dy, (4 - dz) % 4] * R + d % R


def halves(value):
    high = value.astype(BF16)
    return high, (value - high.astype(F32)).astype(BF16)


def times(value, high, low):
    a, b = halves(value)
    total = lax.dot_general(a, high, NT, preferred_element_type=F32)
    total = total + lax.dot_general(b, high, NT, preferred_element_type=F32)
    return total + lax.dot_general(a, low, NT, preferred_element_type=F32)


def kernel(
    dims,
    v_hbm, r_hbm, v_tail, r_tail, factor,
    out,
    v_loc, r_loc, v_all, r_all, p_send, p_recv, g_send, g_recv, g_own, g_all, s_own, s_all, f_high, f_low,
    ld_sem, own_sem, r_ssem, r_rsem, x_ssem, v_ssem, v_rsem,
    gs_ssem, gs_rsem, ga_ssem, ga_rsem, ps_ssem, ps_rsem, sa_ssem, sa_rsem, o_ssem, o_rsem, o_own,
):
    rows, panel, whole, valid, chunk, step = dims
    per = rows // R
    share = panel // (X * Q)
    half = chunk // 2
    prow, pcol = lax.axis_index("prow"), lax.axis_index("pcol")
    x, yl, z = pcol // Q, lax.rem(pcol // Z, YL), lax.rem(pcol, Z)
    h, k = prow // 2, lax.rem(prow, 2)

    yls = [yl, 1 - yl]
    zs = [z] + [lax.rem(z + dz, Z) for dz in range(1, Z)]
    xs = [x] + [lax.rem(x + dx, X) for dx in range(1, X)]
    prows = [prow, h * 2 + 1 - k, (1 - h) * 2 + k, (1 - h) * 2 + 1 - k]

    def at(d, dx=0):
        dy, dz = ORDER[d // R]
        return prows[d % R], xs[dx] * Q + yls[dy] * Z + zs[dz]

    def send(src, dst, ssem, rsem, to):
        copy = pltpu.make_async_remote_copy(
            src_ref=src, dst_ref=dst, send_sem=ssem, recv_sem=rsem,
            device_id=to, device_id_type=pl.DeviceIdType.MESH,
        )
        copy.start()
        return copy

    def arrived(ref, sem):
        pltpu.make_async_copy(ref, ref, sem).wait()

    load_r = pltpu.make_async_copy(r_hbm.at[:, :, pl.ds(0, whole)], r_loc.at[:, :, pl.ds(0, whole)], ld_sem.at[0])
    load_v = pltpu.make_async_copy(v_hbm.at[:, pl.ds(0, whole)], v_loc.at[:, pl.ds(0, whole)], ld_sem.at[1])
    load_r.start()
    load_v.start()

    barrier = pltpu.get_barrier_semaphore()
    for d in OTHERS:
        pl.semaphore_signal(barrier, inc=1, device_id=at(d), device_id_type=pl.DeviceIdType.MESH)
    for dx in (1, 3):
        pl.semaphore_signal(barrier, inc=1, device_id=at(0, dx), device_id_type=pl.DeviceIdType.MESH)

    edge = v_loc.shape[1] - whole
    lane = lax.broadcasted_iota(jnp.int32, (rows, 128), 1)
    v_loc[:, whole:] = jnp.zeros((rows, edge), BF16)
    v_loc[:, whole:whole + 128] = jnp.where(lane < valid, v_tail[...].astype(F32), 0.0).astype(BF16)
    lane8 = lax.broadcasted_iota(jnp.int32, (share, 128), 1)
    for p in range(2):
        r_loc[p, :, whole:] = jnp.zeros((share, edge), BF16)
        r_loc[p, :, whole:whole + 128] = jnp.where(lane8 < valid, r_tail[p].astype(F32), 0.0).astype(BF16)

    pl.semaphore_wait(barrier, GROUP - 1 + 2)

    mine = pl.ds(pl.multiple_of(pcol * share, share), share)

    def columns(slot):
        q = lax.rem(at(slot * R)[1], Q)
        return pl.ds(pl.multiple_of(q * chunk, 128), chunk)

    def rows_at(slot, count=1):
        return pl.ds(slot * rows, count * rows)

    load_r.wait()
    own_r = pltpu.make_async_copy(r_loc.at[:, :, columns(0)], r_all.at[:, mine, :], own_sem.at[0])
    own_r.start()
    for slot in range(1, Q):
        d = mirror(slot * R)
        send(r_loc.at[:, :, columns(d // R)], r_all.at[:, mine, :], r_ssem.at[slot], r_rsem.at[slot], at(d))
    load_v.wait()
    own_v = pltpu.make_async_copy(v_loc.at[:, columns(0)], v_all.at[rows_at(0), :], own_sem.at[1])
    own_v.start()

    def v_out(slot):
        d = mirror(slot * R)
        send(v_loc.at[:, columns(d // R)], v_all.at[rows_at(slot), :], v_ssem.at[slot], v_rsem.at[slot], at(d))

    for slot in range(1, Q - HELD):
        v_out(slot)

    def piece(slot, dx, cols=None):
        source = pl.ds(pl.multiple_of(at(slot * R, dx)[1] * share, share), share)
        return r_all.at[:, source, :] if cols is None else r_all.at[:, source, cols]

    parts = (pl.ds(0, half), pl.ds(half, half))

    def spread(slot):
        if slot == 0:
            own_r.wait()
        else:
            arrived(piece(slot, 0), r_rsem.at[slot])
        for dx in (1, 3):
            send(piece(slot, 0), piece(slot, 0), x_ssem.at[dx * Q + slot], r_rsem.at[(4 - dx) * Q + slot], at(0, dx))

    def relay(slot):
        for number, dx in enumerate((1, 3)):
            arrived(piece(slot, dx), r_rsem.at[dx * Q + slot])
            part = piece(slot, dx, parts[number])
            send(part, part, x_ssem.at[2 * number * Q + slot], r_rsem.at[(2 + 2 * number) * Q + slot], at(0, 4 - dx))

    lag = 1
    for slot in range(Q + lag):
        if slot < Q:
            spread(slot)
        if slot >= lag:
            relay(slot - lag)

    f_high[...], f_low[...] = halves(factor[...])
    for slot in range(Q):
        for number in range(2):
            arrived(piece(slot, 2, parts[number]), r_rsem.at[(2 + 2 * number) * Q + slot])

    def summed(a, b, m):
        def one(j, total):
            cols = pl.ds(pl.multiple_of(j * step, 128), step)
            return total + lax.dot_general(a(cols), b(cols), NT, preferred_element_type=F32)
        return lax.fori_loop(0, chunk // step, one, jnp.zeros((m, panel), F32))

    part = panel // GROUP
    gram = summed(lambda cols: r_all[0, :, cols], lambda cols: r_all[1, :, cols], panel)
    g_send[...] = gram.reshape(GROUP, part, panel).astype(BF16)

    def owner(d):
        across, far = at(d)
        return lax.rem(far, Q) * R + across

    for d in OTHERS:
        send(g_send.at[owner(d)], g_recv.at[mirror(d)], gs_ssem.at[d], gs_rsem.at[mirror(d)], at(d))
    for slot in range(Q - HELD, Q):
        v_out(slot)

    def own_rows(slot, across):
        return pl.ds(pl.multiple_of(slot * rows + across * per, per), per)

    def products(first, count):
        for p in range(2):
            total = summed(lambda cols: v_all[rows_at(first, count), cols], lambda cols: r_all[p, :, cols], rows * count)
            p_send[rows_at(first, count), p * panel:(p + 1) * panel] = total.astype(BF16)
        for d in range(max(first * R, 1), (first + count) * R):
            send(p_send.at[own_rows(d // R, prows[d % R]), :], p_recv.at[mirror(d)], ps_ssem.at[d],
                 ps_rsem.at[mirror(d)], at(d))

    own_v.wait()
    for slot in range(1, 4):
        arrived(v_all.at[rows_at(slot), :], v_rsem.at[slot])
    products(0, 4)

    for d in OTHERS:
        arrived(g_recv.at[d], gs_rsem.at[d])
    g_own[...] = (jnp.sum(g_recv[1:].astype(F32), axis=0) + g_send[owner(0)].astype(F32)).astype(BF16)
    for d in OTHERS:
        send(g_own, g_all.at[owner(0)], ga_ssem.at[d], ga_rsem.at[mirror(d)], at(d))
    g_all[owner(0)] = g_own[...]

    for slot in range(4, Q):
        arrived(v_all.at[rows_at(slot), :], v_rsem.at[slot])
    products(4, 4)

    for d in OTHERS:
        arrived(g_all.at[owner(d)], ga_rsem.at[d])
    for d in OTHERS:
        arrived(p_recv.at[d], ps_rsem.at[d])

    product = p_send[own_rows(0, prow), :].astype(F32)
    product = product + jnp.sum(p_recv[1:].astype(F32), axis=0)
    first = times(product[:, :panel], f_high[0], f_low[0]).astype(BF16)
    second = times(product[:, panel:], f_high[1], f_low[1])
    gram = g_all[...].reshape(panel, panel)
    second = second - times(jnp.dot(first, gram, preferred_element_type=F32), f_high[1], f_low[1])
    s_own[:, :panel] = first
    s_own[:, panel:] = second.astype(BF16)

    for d in OTHERS:
        send(s_own, s_all.at[own_rows(mirror(d) // R, prow), :], sa_ssem.at[d], sa_rsem.at[mirror(d)], at(d))
    s_all[own_rows(0, prow), :] = s_own[...]
    for d in OTHERS:
        arrived(s_all.at[own_rows(d // R, prows[d % R]), :], sa_rsem.at[d])

    base = lax.rem(pcol, Q) * chunk
    width = chunk // 6

    @pl.loop(0, chunk // width)
    def _(j):
        there = pl.ds(pl.multiple_of(base + j * width, 128), width)
        here = pl.ds(pl.multiple_of(j * width, 128), width)
        change = jnp.dot(s_all[:, :panel], r_all[0, :, here], preferred_element_type=F32)
        change = change + jnp.dot(s_all[:, panel:], r_all[1, :, here], preferred_element_type=F32)
        v_all[:, here] = (v_all[:, here].astype(F32) - change).astype(BF16)
        for d in OTHERS:
            send(v_all.at[own_rows(d // R, prows[d % R]), here], out.at[prow, :, there], o_ssem.at[d],
                 o_rsem.at[mirror(d)], at(d))
        pltpu.make_async_copy(v_all.at[own_rows(0, prow), here], out.at[prow, :, there], o_own.at[0]).start()

    for slot in range(Q):
        if slot:
            arrived(piece(slot, 0), r_ssem.at[slot])
            arrived(v_all.at[rows_at(slot), :], v_ssem.at[slot])
        for dx in (1, 3):
            arrived(piece(slot, 0), x_ssem.at[dx * Q + slot])
        for number in range(2):
            arrived(piece(slot, 0, parts[number]), x_ssem.at[2 * number * Q + slot])
    piece_rows = out.at[0, :, pl.ds(0, chunk)]
    arrived(piece_rows, o_own.at[0])
    for d in OTHERS:
        arrived(g_own, gs_ssem.at[d])
        arrived(g_own, ga_ssem.at[d])
        arrived(p_recv.at[0], ps_ssem.at[d])
        arrived(s_own, sa_ssem.at[d])
        arrived(piece_rows, o_ssem.at[d])
    for d in OTHERS:
        across, far = at(d)
        there = pl.ds(pl.multiple_of(lax.rem(far, Q) * chunk, 128), chunk)
        arrived(out.at[across, :, there], o_rsem.at[d])


def joined(width, pieces, out, held, line, in_sem, out_sem):
    loads = [pltpu.make_async_copy(pieces.at[r], held.at[r], in_sem.at[r]) for r in range(R)]
    for load in loads:
        load.start()
    stores = []
    rows = held.shape[1]
    for r in range(R):
        loads[r].wait()
        first, shift = r * width // 128 * 128, r * width % 128
        end = (r + 1) * width // 128 * 128
        if shift == 0:
            source = held.at[r, :, pl.ds(0, end - first)]
        else:
            count = (end - first) // 128
            lane = lax.broadcasted_iota(jnp.int32, (rows, 128), 1)
            keep = held[r - 1, :, pl.ds(first - (r - 1) * width // 128 * 128, 128)].astype(F32)
            turned = pltpu.roll(held[r, :, :128].astype(F32), shift, 1)
            line[r // 2, :, :128] = jnp.where(lane < shift, keep, turned).astype(BF16)
            width_step = 13 * 128
            for a in range(128, count * 128, width_step):
                n = min(width_step, count * 128 - a)
                wide = held[r, :, a - 128:a + n].astype(F32)
                line[r // 2, :, a:a + n] = pltpu.roll(wide, shift, 1)[:, 128:].astype(BF16)
            source = line.at[r // 2]
        store = pltpu.make_async_copy(source, out.at[:, pl.ds(first, end - first)], out_sem.at[r])
        store.start()
        stores.append(store)
    for store in stores:
        store.wait()


def body(vectors, reflectors, panel_factor):
    rows, width = vectors.shape
    panel = panel_factor.shape[1]
    share = reflectors.shape[1]
    tiles = pl.cdiv(width, 128)
    chunk = pl.cdiv(tiles, Q) * 128
    whole = (tiles - 1) * 128
    dims = (rows, panel, whole, width - whole, chunk, chunk // 3)
    per = rows // R
    any_spec = pl.BlockSpec(memory_space=pl.ANY)
    dma = pltpu.SemaphoreType.DMA
    part = panel // GROUP
    gathered = pl.pallas_call(
        functools.partial(kernel, dims),
        grid=(1,),
        out_shape=jax.ShapeDtypeStruct((R, per, chunk * Q), BF16),
        in_specs=[
            any_spec, any_spec,
            pl.BlockSpec((rows, 128), lambda i: (0, tiles - 1)),
            pl.BlockSpec((2, share, 128), lambda i: (0, 0, tiles - 1)),
            pl.BlockSpec((2, panel, panel), lambda i: (0, 0, 0)),
        ],
        out_specs=any_spec,
        scratch_shapes=[
            pltpu.VMEM((rows, chunk * Q), BF16),
            pltpu.VMEM((2, share, chunk * Q), BF16),
            pltpu.VMEM((rows * Q, chunk), BF16),
            pltpu.VMEM((2, panel, chunk), BF16),
            pltpu.VMEM((rows * Q, 2 * panel), BF16),
            pltpu.VMEM((GROUP, per, 2 * panel), BF16),
            pltpu.VMEM((GROUP, part, panel), BF16),
            pltpu.VMEM((GROUP, part, panel), BF16),
            pltpu.VMEM((part, panel), BF16),
            pltpu.VMEM((GROUP, part, panel), BF16),
            pltpu.VMEM((per, 2 * panel), BF16),
            pltpu.VMEM((rows * Q, 2 * panel), BF16),
            pltpu.VMEM((2, panel, panel), BF16),
            pltpu.VMEM((2, panel, panel), BF16),
            dma((2,)), dma((2,)), dma((Q,)), dma(((X + 1) * Q,)), dma((X * Q,)), dma((Q,)), dma((Q,)),
            dma((GROUP,)), dma((GROUP,)), dma((GROUP,)), dma((GROUP,)), dma((GROUP,)), dma((GROUP,)),
            dma((GROUP,)), dma((GROUP,)), dma((GROUP,)), dma((GROUP,)), dma((1,)),
        ],
        compiler_params=pltpu.CompilerParams(
            collective_id=0, has_side_effects=True, vmem_limit_bytes=61 * 1024 * 1024
        ),
        name="back_transform",
    )(vectors, reflectors, vectors, reflectors, panel_factor)
    line = R * width // 128 * 128 - (R - 1) * width // 128 * 128
    rows_out = pl.pallas_call(
        functools.partial(joined, width),
        out_shape=jax.ShapeDtypeStruct((per, R * width), BF16),
        in_specs=[any_spec],
        out_specs=any_spec,
        scratch_shapes=[
            pltpu.VMEM((R, per, chunk * Q), BF16), pltpu.VMEM((2, per, line), BF16), dma((R,)), dma((R,)),
        ],
        compiler_params=pltpu.CompilerParams(vmem_limit_bytes=61 * 1024 * 1024),
        name="joined",
    )(gathered)
    return rows_out[None]


def solution(mesh):
    placed = (P("pcol", "prow"), P(None, "pcol", "prow"), P())
    return jax.shard_map(
        body, mesh=mesh, in_specs=placed, out_specs=P("pcol", "prow", None), check_vma=False
    )
```

time: 475 us -> 143 us (0.30)
  waiting for transfers between devices: 312 us -> 0 us
  Pallas kernels: 0 us -> 143 us
  blocking collectives: 95 us -> 0 us
  matrix products: 42.6 us -> 0 us
  between operations: 13.4 us -> 0.01 us
  local copies, waits for them, and re-layouts: 11.7 us -> 0 us
    all_gather x2 -> x0, waiting for transfers between devices: 311 us -> none  [body(): single = lax.all_gather(reflectors[number], 'pcol', axis=0, tiled=True)]
    pallas_call x0 -> x2, Pallas kernels: none -> 143 us  [the longest x1 139 us: body(): pl.pallas_call(functools.partial(kernel, dims), grid=(1,), out_shape=jax....]
    all_to_all x1 -> x0, blocking collectives: 49 us -> none  [body(): lax.all_to_all(current, 'prow', split_axis=0, concat_axis=1, tiled=True)]
    all_gather x2 -> x0, blocking collectives: 46 us -> none  [over_pieces(): return lax.all_gather(value, axis).astype(jnp.float32).sum(0)]
    dot_general x6 -> x0, matrix products: 42.6 us -> none  [the longest x2 22.5 us: partial_products(): lax.dot_general(current, panel, (((1,), (1,)), ((), ())), preferred_eleme...]
    broadcast_in_dim x1 -> x0, local copies, waits for them, and re-layouts: 6.17 us -> none  [body(): return owned_rows[None]]
  transfers between devices with their start and end apart: 2 -> 0, of which waited for: 2 -> 0; matrix products, arithmetic and copies ran while one was open for 5% -> 0% of each run, Pallas kernels for 0% -> 0%
where the time goes in v3:
time: 143 us
  Pallas kernels  143 us (100%)
    pallas_call x1, Pallas kernels, body(): pl.pallas_call(functools.partial(kernel, dims), grid=(1,), out_shape=jax....  139 us
    pallas_call x1, Pallas kernels, body(): pl.pallas_call(functools.partial(joined, width), out_shape=jax.ShapeDtype...  3.48 us

profile of v3, /device:TPU:1, one launch (start us, length us, event | category | flops | bytes accessed | tf_op | source)
XLA Modules:
  0.0 142.6 jit_solution(14331678753823056115)
XLA Ops:
  0.0 139.1 %back_transform.1.pieces = bf16[4,16,30720]{2,1,0:T(8,128)(2,1)} custom-call(bf16[64,30016]{1,0:T(8,128)(2,1)} %v_tail.1, bf16[2,8,30016]{2,1,0:T(8,128)(2,1)} %r_tail.1, bf16[64,30016]{1,0:T(8,128)(2,1)} %v_tail.1, bf16[2,8,30016]{2,1,0:T(8,128)(2,1)} %r_tail.1, f32[2,256,256]{2,1,0:T(8,128)} %factor.1), custom_call_target="tpu_custom_call" | custom-call | tf_op jit(solution)/shard_map/back_transform/pallas_call | solution.py:300
  139.1 3.5 %joined.1 = bf16[16,120064]{1,0:T(8,128)(2,1)} custom-call(bf16[4,16,30720]{2,1,0:T(8,128)(2,1)} %back_transform.1.pieces), custom_call_target="tpu_custom_call" | custom-call | tf_op jit(solution)/shard_map/joined/pallas_call | solution.py:336

commit v4 on v3

--- a/solution.py
+++ b/solution.py
@@ -10,10 +10,40 @@
 X, YL, Z, R = 4, 2, 4, 4
 Q = YL * Z
 GROUP = Q * R
-ORDER = ((0, 0), (0, 3), (0, 1), (1, 3), (1, 1), (0, 2), (1, 2), (1, 0))
+ORDER = ((0, 0), (1, 0), (1, 1), (1, 3), (0, 2), (1, 2), (0, 1), (0, 3))
 SLOT = {pair: number for number, pair in enumerate(ORDER)}
-OTHERS = range(1, GROUP)
-HELD = 0
+LATE, THIRDS = Q // 2, 3
+
+
+def hops(d):
+    dy, dz = ORDER[d // R]
+    return min(dz, Z - dz) + (1 if dy else d % R // 2 * 2)
+
+
+OTHERS = sorted(range(1, GROUP), key=lambda d: -hops(d))
+
+TURNS = (
+    (
+        ((0, 1, 2),),
+        ((0, 1, 1), (0, 1, 3), (0, 0, 1), (0, 0, 3)),
+        ((1, 0, 1), (1, 1, 3)),
+        ((1, 0, 3), (1, 1, 1)),
+        ((1, 0, 2), (1, 1, 2), (1, 0, 0), (1, 1, 0)),
+        ((0, 1, 0), (0, 0, 2)),
+    ),
+    (
+        ((1, 0, 0), (1, 1, 0), (1, 0, 2), (1, 1, 2)),
+        ((1, 0, 1), (1, 1, 3)),
+        ((1, 0, 3), (1, 1, 1)),
+        ((0, 1, 2),),
+        ((0, 1, 0), (0, 0, 2)),
+        ((0, 1, 1), (0, 1, 3), (0, 0, 1), (0, 0, 3)),
+    ),
+)
+LEAVING = [
+    [SLOT[lo, dz] * R + hi * 2 + core for turn in turns for core in (0, 1) for lo, hi, dz in turn] + [1]
+    for turns in TURNS
+]
 BF16, F32 = jnp.bfloat16, jnp.float32
 NT = (((1,), (1,)), ((), ()))
 
@@ -39,7 +69,7 @@
     dims,
     v_hbm, r_hbm, v_tail, r_tail, factor,
     out,
-    v_loc, r_loc, v_all, r_all, p_send, p_recv, g_send, g_recv, g_own, g_all, s_own, s_all, f_high, f_low,
+    v_loc, r_loc, v_all, r_all, p_sum, p_send, p_recv, g_send, g_recv, g_own, g_all, s_own, s_all, f_high, f_low,
     ld_sem, own_sem, r_ssem, r_rsem, x_ssem, v_ssem, v_rsem,
     gs_ssem, gs_rsem, ga_ssem, ga_rsem, ps_ssem, ps_rsem, sa_ssem, sa_rsem, o_ssem, o_rsem, o_own,
 ):
@@ -112,12 +142,26 @@
     own_v = pltpu.make_async_copy(v_loc.at[:, columns(0)], v_all.at[rows_at(0), :], own_sem.at[1])
     own_v.start()
 
-    def v_out(slot):
+    third = chunk // THIRDS
+
+    def v_sem(slot, number):
+        return slot if number is None else Q + slot * THIRDS + number
+
+    def v_landing(slot, number=None):
+        return v_all.at[rows_at(slot), pl.ds(0, chunk) if number is None else pl.ds(number * third, third)]
+
+    def v_out(slot, number=None):
         d = mirror(slot * R)
-        send(v_loc.at[:, columns(d // R)], v_all.at[rows_at(slot), :], v_ssem.at[slot], v_rsem.at[slot], at(d))
-
-    for slot in range(1, Q - HELD):
+        first = lax.rem(at(d)[1], Q) * chunk + (number or 0) * third
+        source = v_loc.at[:, pl.ds(pl.multiple_of(first, 128), chunk if number is None else third)]
+        sem = v_sem(slot, number)
+        send(source, v_landing(slot, number), v_ssem.at[sem], v_rsem.at[sem], at(d))
+
+    for slot in range(LATE, Q):
         v_out(slot)
+    for number in range(THIRDS - 1):
+        for slot in range(1, LATE):
+            v_out(slot, number)
 
     def piece(slot, dx, cols=None):
         source = pl.ds(pl.multiple_of(at(slot * R, dx)[1] * share, share), share)
@@ -167,35 +211,47 @@
 
     for d in OTHERS:
         send(g_send.at[owner(d)], g_recv.at[mirror(d)], gs_ssem.at[d], gs_rsem.at[mirror(d)], at(d))
-    for slot in range(Q - HELD, Q):
-        v_out(slot)
+    for slot in range(1, LATE):
+        v_out(slot, THIRDS - 1)
 
     def own_rows(slot, across):
         return pl.ds(pl.multiple_of(slot * rows + across * per, per), per)
 
-    def products(first, count):
-        for p in range(2):
-            total = summed(lambda cols: v_all[rows_at(first, count), cols], lambda cols: r_all[p, :, cols], rows * count)
-            p_send[rows_at(first, count), p * panel:(p + 1) * panel] = total.astype(BF16)
-        for d in range(max(first * R, 1), (first + count) * R):
+    def p_out(first, count):
+        for d in [d for d in OTHERS if first <= d // R < first + count]:
             send(p_send.at[own_rows(d // R, prows[d % R]), :], p_recv.at[mirror(d)], ps_ssem.at[d],
                  ps_rsem.at[mirror(d)], at(d))
 
+    for slot in range(LATE, Q):
+        arrived(v_landing(slot), v_rsem.at[slot])
+    for p in range(2):
+        total = summed(lambda cols: v_all[rows_at(LATE, Q - LATE), cols], lambda cols: r_all[p, :, cols], rows * (Q - LATE))
+        p_send[rows_at(LATE, Q - LATE), p * panel:(p + 1) * panel] = total.astype(BF16)
+    p_out(LATE, Q - LATE)
     own_v.wait()
-    for slot in range(1, 4):
-        arrived(v_all.at[rows_at(slot), :], v_rsem.at[slot])
-    products(0, 4)
-
-    for d in OTHERS:
-        arrived(g_recv.at[d], gs_rsem.at[d])
-    g_own[...] = (jnp.sum(g_recv[1:].astype(F32), axis=0) + g_send[owner(0)].astype(F32)).astype(BF16)
-    for d in OTHERS:
-        send(g_own, g_all.at[owner(0)], ga_ssem.at[d], ga_rsem.at[mirror(d)], at(d))
-    g_all[owner(0)] = g_own[...]
-
-    for slot in range(4, Q):
-        arrived(v_all.at[rows_at(slot), :], v_rsem.at[slot])
-    products(4, 4)
+
+    for number in range(THIRDS):
+        if number == THIRDS - 1:
+            for d in OTHERS:
+                arrived(g_recv.at[d], gs_rsem.at[d])
+            g_own[...] = (jnp.sum(g_recv[1:].astype(F32), axis=0) + g_send[owner(0)].astype(F32)).astype(BF16)
+            for d in OTHERS:
+                send(g_own, g_all.at[owner(0)], ga_ssem.at[d], ga_rsem.at[mirror(d)], at(d))
+            g_all[owner(0)] = g_own[...]
+        for slot in range(1, LATE):
+            arrived(v_landing(slot, number), v_rsem.at[v_sem(slot, number)])
+        cols = pl.ds(number * third, third)
+        for p in range(2):
+            here = slice(p * panel, (p + 1) * panel)
+            total = lax.dot_general(
+                v_all[rows_at(0, LATE), cols], r_all[p, :, cols], NT, preferred_element_type=F32)
+            if number:
+                total = total + p_sum[:, here]
+            if number < THIRDS - 1:
+                p_sum[:, here] = total
+            else:
+                p_send[rows_at(0, LATE), here] = total.astype(BF16)
+    p_out(0, LATE)
 
     for d in OTHERS:
         arrived(g_all.at[owner(d)], ga_rsem.at[d])
@@ -211,11 +267,18 @@
     s_own[:, :panel] = first
     s_own[:, panel:] = second.astype(BF16)
 
-    for d in OTHERS:
+    def s_place(d):
+        return s_all.at[own_rows(d // R, prows[d % R]), :]
+
+    for d in [d for d in OTHERS if d % 2 == 0]:
         send(s_own, s_all.at[own_rows(mirror(d) // R, prow), :], sa_ssem.at[d], sa_rsem.at[mirror(d)], at(d))
+    send(s_own, s_place(0), sa_ssem.at[1], sa_rsem.at[1], at(1))
     s_all[own_rows(0, prow), :] = s_own[...]
-    for d in OTHERS:
-        arrived(s_all.at[own_rows(d // R, prows[d % R]), :], sa_rsem.at[d])
+    for d in [d for d in OTHERS if d % 2 == 0]:
+        arrived(s_place(d), sa_rsem.at[d])
+        send(s_place(d), s_place(d), sa_ssem.at[d + 1], sa_rsem.at[d + 1], at(1))
+    for d in range(1, GROUP, 2):
+        arrived(s_place(d), sa_rsem.at[d])
 
     base = lax.rem(pcol, Q) * chunk
     width = chunk // 6
@@ -227,15 +290,19 @@
         change = jnp.dot(s_all[:, :panel], r_all[0, :, here], preferred_element_type=F32)
         change = change + jnp.dot(s_all[:, panel:], r_all[1, :, here], preferred_element_type=F32)
         v_all[:, here] = (v_all[:, here].astype(F32) - change).astype(BF16)
-        for d in OTHERS:
-            send(v_all.at[own_rows(d // R, prows[d % R]), here], out.at[prow, :, there], o_ssem.at[d],
-                 o_rsem.at[mirror(d)], at(d))
+        for core in range(2):
+            @pl.when(k == core)
+            def _():
+                for d in LEAVING[core]:
+                    send(v_all.at[own_rows(d // R, prows[d % R]), here], out.at[prow, :, there], o_ssem.at[d],
+                         o_rsem.at[mirror(d)], at(d))
         pltpu.make_async_copy(v_all.at[own_rows(0, prow), here], out.at[prow, :, there], o_own.at[0]).start()
 
     for slot in range(Q):
         if slot:
             arrived(piece(slot, 0), r_ssem.at[slot])
-            arrived(v_all.at[rows_at(slot), :], v_ssem.at[slot])
+        for number in ((None,) if slot >= LATE else range(THIRDS) if slot else ()):
+            arrived(v_landing(slot, number), v_ssem.at[v_sem(slot, number)])
         for dx in (1, 3):
             arrived(piece(slot, 0), x_ssem.at[dx * Q + slot])
         for number in range(2):
@@ -313,6 +380,7 @@
             pltpu.VMEM((2, share, chunk * Q), BF16),
             pltpu.VMEM((rows * Q, chunk), BF16),
             pltpu.VMEM((2, panel, chunk), BF16),
+            pltpu.VMEM((rows * LATE, 2 * panel), F32),
             pltpu.VMEM((rows * Q, 2 * panel), BF16),
             pltpu.VMEM((GROUP, per, 2 * panel), BF16),
             pltpu.VMEM((GROUP, part, panel), BF16),
@@ -323,7 +391,7 @@
             pltpu.VMEM((rows * Q, 2 * panel), BF16),
             pltpu.VMEM((2, panel, panel), BF16),
             pltpu.VMEM((2, panel, panel), BF16),
-            dma((2,)), dma((2,)), dma((Q,)), dma(((X + 1) * Q,)), dma((X * Q,)), dma((Q,)), dma((Q,)),
+            dma((2,)), dma((2,)), dma((Q,)), dma(((X + 1) * Q,)), dma((X * Q,)), dma((Q + LATE * THIRDS,)), dma((Q + LATE * THIRDS,)),
             dma((GROUP,)), dma((GROUP,)), dma((GROUP,)), dma((GROUP,)), dma((GROUP,)), dma((GROUP,)),
             dma((GROUP,)), dma((GROUP,)), dma((GROUP,)), dma((GROUP,)), dma((1,)),
         ],

time: 143 us -> 138 us (0.965)
  Pallas kernels: 143 us -> 137 us
    pallas_call x1, Pallas kernels: 139 us -> 134 us  [body(): pl.pallas_call(functools.partial(kernel, dims), grid=(1,), out_shape=jax....]
where the time goes in v4:
time: 138 us; the launch traced here: 137 us
  Pallas kernels  137 us (99%)
    pallas_call x1, Pallas kernels, body(): pl.pallas_call(functools.partial(kernel, dims), grid=(1,), out_shape=jax....  134 us
    pallas_call x1, Pallas kernels, body(): pl.pallas_call(functools.partial(joined, width), out_shape=jax.ShapeDtype...  3.48 us

profile of v4, /device:TPU:1, one launch (start us, length us, event | category | flops | bytes accessed | tf_op | source)
XLA Modules:
  0.0 137.5 jit_solution(10513884087441679731)
XLA Ops:
  0.0 134.0 %back_transform.1.pieces = bf16[4,16,30720]{2,1,0:T(8,128)(2,1)} custom-call(bf16[64,30016]{1,0:T(8,128)(2,1)} %v_tail.1, bf16[2,8,30016]{2,1,0:T(8,128)(2,1)} %r_tail.1, bf16[64,30016]{1,0:T(8,128)(2,1)} %v_tail.1, bf16[2,8,30016]{2,1,0:T(8,128)(2,1)} %r_tail.1, f32[2,256,256]{2,1,0:T(8,128)} %factor.1), custom_call_target="tpu_custom_call" | custom-call | tf_op jit(solution)/shard_map/back_transform/pallas_call | solution.py:367
  134.0 3.5 %joined.1 = bf16[16,120064]{1,0:T(8,128)(2,1)} custom-call(bf16[4,16,30720]{2,1,0:T(8,128)(2,1)} %back_transform.1.pieces), custom_call_target="tpu_custom_call" | custom-call | tf_op jit(solution)/shard_map/joined/pallas_call | solution.py:404

commit v5 on v3

--- a/solution.py
+++ b/solution.py
@@ -10,10 +10,40 @@
 X, YL, Z, R = 4, 2, 4, 4
 Q = YL * Z
 GROUP = Q * R
-ORDER = ((0, 0), (0, 3), (0, 1), (1, 3), (1, 1), (0, 2), (1, 2), (1, 0))
+ORDER = ((0, 0), (1, 0), (1, 1), (1, 3), (0, 2), (1, 2), (0, 1), (0, 3))
 SLOT = {pair: number for number, pair in enumerate(ORDER)}
-OTHERS = range(1, GROUP)
-HELD = 0
+PAIRS = [(slot, flip) for slot in range(Q) for flip in range(2)]
+PIECES, AHEAD = 5, (2, 3, 4, 5)
+GOING = ((1, 2), (1, 0), (0, 2), (1, 1), (0, 3), (1, 3), (0, 1))
+
+
+def hops(d):
+    dy, dz = ORDER[d // R]
+    return min(dz, Z - dz) + (1 if dy else d % R // 2 * 2)
+
+
+OTHERS = sorted(range(1, GROUP), key=lambda d: -hops(d))
+
+TURNS = (
+    (
+        ((0, 1, 2),),
+        ((0, 1, 1), (0, 1, 3), (0, 0, 1), (0, 0, 3)),
+        ((1, 0, 1), (1, 1, 3)),
+        ((1, 0, 3), (1, 1, 1)),
+        ((1, 0, 2), (1, 1, 2), (1, 0, 0), (1, 1, 0)),
+        ((0, 1, 0), (0, 0, 2)),
+    ),
+    (
+        ((1, 0, 0), (1, 1, 0), (1, 0, 2), (1, 1, 2)),
+        ((1, 0, 1), (1, 1, 3)),
+        ((1, 0, 3), (1, 1, 1)),
+        ((0, 1, 2),),
+        ((0, 1, 0), (0, 0, 2)),
+        ((0, 1, 1), (0, 1, 3), (0, 0, 1), (0, 0, 3)),
+    ),
+)
+LEAVING = [[(SLOT[lo, dz], hi) for turn in turns for lo, hi, dz in turn] for turns in TURNS]
+FAR = sorted(PAIRS[1:], key=lambda pair: -hops(pair[0] * R + pair[1] * 2))
 BF16, F32 = jnp.bfloat16, jnp.float32
 NT = (((1,), (1,)), ((), ()))
 
@@ -39,7 +69,7 @@
     dims,
     v_hbm, r_hbm, v_tail, r_tail, factor,
     out,
-    v_loc, r_loc, v_all, r_all, p_send, p_recv, g_send, g_recv, g_own, g_all, s_own, s_all, f_high, f_low,
+    v_loc, r_loc, v_all, r_all, p_sum, p_send, p_recv, g_send, g_recv, g_own, g_all, s_own, s_all, f_high, f_low,
     ld_sem, own_sem, r_ssem, r_rsem, x_ssem, v_ssem, v_rsem,
     gs_ssem, gs_rsem, ga_ssem, ga_rsem, ps_ssem, ps_rsem, sa_ssem, sa_rsem, o_ssem, o_rsem, o_own,
 ):
@@ -72,9 +102,14 @@
         pltpu.make_async_copy(ref, ref, sem).wait()
 
     load_r = pltpu.make_async_copy(r_hbm.at[:, :, pl.ds(0, whole)], r_loc.at[:, :, pl.ds(0, whole)], ld_sem.at[0])
-    load_v = pltpu.make_async_copy(v_hbm.at[:, pl.ds(0, whole)], v_loc.at[:, pl.ds(0, whole)], ld_sem.at[1])
+    load_v = [
+        pltpu.make_async_copy(
+            v_hbm.at[pl.ds(r * per, per), pl.ds(0, whole)], v_loc.at[r // 2, r % 2, :, pl.ds(0, whole)], ld_sem.at[1 + r])
+        for r in (0, 2, 1, 3)
+    ]
     load_r.start()
-    load_v.start()
+    for load in load_v:
+        load.start()
 
     barrier = pltpu.get_barrier_semaphore()
     for d in OTHERS:
@@ -82,10 +117,12 @@
     for dx in (1, 3):
         pl.semaphore_signal(barrier, inc=1, device_id=at(0, dx), device_id_type=pl.DeviceIdType.MESH)
 
-    edge = v_loc.shape[1] - whole
+    edge = v_loc.shape[3] - whole
     lane = lax.broadcasted_iota(jnp.int32, (rows, 128), 1)
-    v_loc[:, whole:] = jnp.zeros((rows, edge), BF16)
-    v_loc[:, whole:whole + 128] = jnp.where(lane < valid, v_tail[...].astype(F32), 0.0).astype(BF16)
+    tail = jnp.where(lane < valid, v_tail[...].astype(F32), 0.0).astype(BF16)
+    for r in range(R):
+        v_loc[r // 2, r % 2, :, whole:] = jnp.zeros((per, edge), BF16)
+        v_loc[r // 2, r % 2, :, whole:whole + 128] = tail[r * per:(r + 1) * per]
     lane8 = lax.broadcasted_iota(jnp.int32, (share, 128), 1)
     for p in range(2):
         r_loc[p, :, whole:] = jnp.zeros((share, edge), BF16)
@@ -98,9 +135,6 @@
     def columns(slot):
         q = lax.rem(at(slot * R)[1], Q)
         return pl.ds(pl.multiple_of(q * chunk, 128), chunk)
-
-    def rows_at(slot, count=1):
-        return pl.ds(slot * rows, count * rows)
 
     load_r.wait()
     own_r = pltpu.make_async_copy(r_loc.at[:, :, columns(0)], r_all.at[:, mine, :], own_sem.at[0])
@@ -108,16 +142,39 @@
     for slot in range(1, Q):
         d = mirror(slot * R)
         send(r_loc.at[:, :, columns(d // R)], r_all.at[:, mine, :], r_ssem.at[slot], r_rsem.at[slot], at(d))
-    load_v.wait()
-    own_v = pltpu.make_async_copy(v_loc.at[:, columns(0)], v_all.at[rows_at(0), :], own_sem.at[1])
-    own_v.start()
-
-    def v_out(slot):
-        d = mirror(slot * R)
-        send(v_loc.at[:, columns(d // R)], v_all.at[rows_at(slot), :], v_ssem.at[slot], v_rsem.at[slot], at(d))
-
-    for slot in range(1, Q - HELD):
-        v_out(slot)
+    part_width = chunk // PIECES
+
+    def v_sem(slot, number):
+        return slot if number is None else Q + slot * PIECES + number
+
+    def v_landing(slot, number=None):
+        if number is None:
+            return v_all.at[0, slot]
+        return v_all.at[1, slot, :, :, pl.ds(number * part_width, part_width)]
+
+    def v_source(slot, number):
+        first = lax.rem(at(slot * R)[1], Q) * chunk + (number or 0) * part_width
+        width = chunk if number is None else part_width
+        return v_loc.at[:, 0 if number is None else 1, :, pl.ds(pl.multiple_of(first, 128), width)]
+
+    def v_out(numbers):
+        for number in numbers:
+            for pair in GOING:
+                d = SLOT[pair] * R
+                slot = mirror(d) // R
+                sem = v_sem(slot, number)
+                send(v_source(d // R, number), v_landing(slot, number), v_ssem.at[sem], v_rsem.at[sem], at(d))
+
+    load_v[0].wait()
+    load_v[1].wait()
+    v_out([None])
+    own_first = pltpu.make_async_copy(v_source(0, None), v_landing(0), own_sem.at[1])
+    own_first.start()
+    load_v[2].wait()
+    load_v[3].wait()
+    v_out(range(AHEAD[0]))
+    own_second = pltpu.make_async_copy(v_loc.at[:, 1, :, columns(0)], v_all.at[1, 0], own_sem.at[2])
+    own_second.start()
 
     def piece(slot, dx, cols=None):
         source = pl.ds(pl.multiple_of(at(slot * R, dx)[1] * share, share), share)
@@ -167,24 +224,41 @@
 
     for d in OTHERS:
         send(g_send.at[owner(d)], g_recv.at[mirror(d)], gs_ssem.at[d], gs_rsem.at[mirror(d)], at(d))
-    for slot in range(Q - HELD, Q):
-        v_out(slot)
-
-    def own_rows(slot, across):
-        return pl.ds(pl.multiple_of(slot * rows + across * per, per), per)
-
-    def products(first, count):
-        for p in range(2):
-            total = summed(lambda cols: v_all[rows_at(first, count), cols], lambda cols: r_all[p, :, cols], rows * count)
-            p_send[rows_at(first, count), p * panel:(p + 1) * panel] = total.astype(BF16)
-        for d in range(max(first * R, 1), (first + count) * R):
-            send(p_send.at[own_rows(d // R, prows[d % R]), :], p_recv.at[mirror(d)], ps_ssem.at[d],
-                 ps_rsem.at[mirror(d)], at(d))
-
-    own_v.wait()
-    for slot in range(1, 4):
-        arrived(v_all.at[rows_at(slot), :], v_rsem.at[slot])
-    products(0, 4)
+    v_out(range(AHEAD[0], AHEAD[1]))
+
+    sides = (h, 1 - h)
+
+    def place(slot, flip, core):
+        return sides[flip] * 2 + core, at(slot * R)[1]
+
+    def turned(slot):
+        return mirror(slot * R) // R
+
+    def tall(ref):
+        value = ref[...]
+        return value.reshape(2 * Q * per, value.shape[-1])
+
+    def p_out(core):
+        for slot, flip in FAR:
+            send(p_send.at[core, slot, sides[flip]], p_recv.at[(turned(slot) * 2 + flip) * 2 + k],
+                 ps_ssem.at[(slot * 2 + flip) * 2 + core], ps_rsem.at[(turned(slot) * 2 + flip) * 2 + k], place(slot, flip, core))
+
+        @pl.when(k != core)
+        def _():
+            send(p_send.at[core, 0, h], p_recv.at[k], ps_ssem.at[core], ps_rsem.at[k], place(0, 0, core))
+
+        @pl.when(k == core)
+        def _():
+            p_recv[k] = p_send[core, 0, h]
+
+    for slot in range(1, Q):
+        arrived(v_landing(slot), v_rsem.at[slot])
+    own_first.wait()
+    for p in range(2):
+        total = summed(lambda cols: tall(v_all.at[0, :, :, :, cols]), lambda cols: r_all[p, :, cols], 2 * Q * per)
+        p_send[0, :, :, :, p * panel:(p + 1) * panel] = total.astype(BF16).reshape(Q, 2, per, panel)
+    p_out(0)
+    v_out(range(AHEAD[1], AHEAD[2]))
 
     for d in OTHERS:
         arrived(g_recv.at[d], gs_rsem.at[d])
@@ -192,50 +266,110 @@
     for d in OTHERS:
         send(g_own, g_all.at[owner(0)], ga_ssem.at[d], ga_rsem.at[mirror(d)], at(d))
     g_all[owner(0)] = g_own[...]
-
-    for slot in range(4, Q):
-        arrived(v_all.at[rows_at(slot), :], v_rsem.at[slot])
-    products(4, 4)
-
-    for d in OTHERS:
-        arrived(g_all.at[owner(d)], ga_rsem.at[d])
-    for d in OTHERS:
-        arrived(p_recv.at[d], ps_rsem.at[d])
-
-    product = p_send[own_rows(0, prow), :].astype(F32)
-    product = product + jnp.sum(p_recv[1:].astype(F32), axis=0)
-    first = times(product[:, :panel], f_high[0], f_low[0]).astype(BF16)
-    second = times(product[:, panel:], f_high[1], f_low[1])
-    gram = g_all[...].reshape(panel, panel)
-    second = second - times(jnp.dot(first, gram, preferred_element_type=F32), f_high[1], f_low[1])
-    s_own[:, :panel] = first
-    s_own[:, panel:] = second.astype(BF16)
-
-    for d in OTHERS:
-        send(s_own, s_all.at[own_rows(mirror(d) // R, prow), :], sa_ssem.at[d], sa_rsem.at[mirror(d)], at(d))
-    s_all[own_rows(0, prow), :] = s_own[...]
-    for d in OTHERS:
-        arrived(s_all.at[own_rows(d // R, prows[d % R]), :], sa_rsem.at[d])
+    v_out(range(AHEAD[2], AHEAD[3]))
+
+    def second_half(numbers):
+        for number in numbers:
+            for slot in range(1, Q):
+                arrived(v_landing(slot, number), v_rsem.at[v_sem(slot, number)])
+            cols = pl.ds(number * part_width, part_width)
+            for p in range(2):
+                here = slice(p * panel, (p + 1) * panel)
+                total = lax.dot_general(
+                    tall(v_all.at[1, :, :, :, cols]), r_all[p, :, cols], NT, preferred_element_type=F32)
+                if number:
+                    total = total + p_sum[:, here]
+                if number < PIECES - 1:
+                    p_sum[:, here] = total
+                else:
+                    p_send[1, :, :, :, here] = total.astype(BF16).reshape(Q, 2, per, panel)
+
+    own_second.wait()
+    second_half(range(AHEAD[1]))
+
+    def s_place(core, slot, flip):
+        return s_all.at[core, slot, sides[flip]]
+
+    def s_out(core):
+        @pl.when(k == core)
+        def _():
+            for slot, flip in FAR:
+                for sender in range(2):
+                    spot = (slot * 2 + flip) * 2 + sender
+                    arrived(p_recv.at[spot], ps_rsem.at[spot])
+            arrived(p_recv.at[1 - k], ps_rsem.at[1 - k])
+            product = jnp.sum(p_recv[...].astype(F32), axis=0)
+            first = times(product[:, :panel], f_high[0], f_low[0]).astype(BF16)
+            second = times(product[:, panel:], f_high[1], f_low[1])
+            for d in OTHERS:
+                arrived(g_all.at[owner(d)], ga_rsem.at[d])
+            gram = g_all[...].reshape(panel, panel)
+            second = second - times(jnp.dot(first, gram, preferred_element_type=F32), f_high[1], f_low[1])
+            s_own[:, :panel] = first
+            s_own[:, panel:] = second.astype(BF16)
+            for slot, flip in FAR:
+                spot = (turned(slot) * 2 + flip) * 2 + core
+                send(s_own, s_all.at[core, turned(slot), h], sa_ssem.at[(slot * 2 + flip) * 2], sa_rsem.at[spot],
+                     place(slot, flip, core))
+            send(s_own, s_place(core, 0, 0), sa_ssem.at[1], sa_rsem.at[core], place(0, 0, 1 - core))
+            s_all[core, 0, h] = s_own[...]
+
+    def s_shared(core):
+        @pl.when(k == core)
+        def _():
+            for slot, flip in FAR:
+                spot = (slot * 2 + flip) * 2 + core
+                arrived(s_place(core, slot, flip), sa_rsem.at[spot])
+                send(s_place(core, slot, flip), s_place(core, slot, flip), sa_ssem.at[(slot * 2 + flip) * 2 + 1],
+                     sa_rsem.at[spot], place(0, 0, 1 - core))
+
+        @pl.when(k != core)
+        def _():
+            for slot, flip in FAR + [(0, 0)]:
+                arrived(s_place(core, slot, flip), sa_rsem.at[(slot * 2 + flip) * 2 + core])
 
     base = lax.rem(pcol, Q) * chunk
     width = chunk // 6
 
-    @pl.loop(0, chunk // width)
-    def _(j):
-        there = pl.ds(pl.multiple_of(base + j * width, 128), width)
-        here = pl.ds(pl.multiple_of(j * width, 128), width)
-        change = jnp.dot(s_all[:, :panel], r_all[0, :, here], preferred_element_type=F32)
-        change = change + jnp.dot(s_all[:, panel:], r_all[1, :, here], preferred_element_type=F32)
-        v_all[:, here] = (v_all[:, here].astype(F32) - change).astype(BF16)
-        for d in OTHERS:
-            send(v_all.at[own_rows(d // R, prows[d % R]), here], out.at[prow, :, there], o_ssem.at[d],
-                 o_rsem.at[mirror(d)], at(d))
-        pltpu.make_async_copy(v_all.at[own_rows(0, prow), here], out.at[prow, :, there], o_own.at[0]).start()
+    def results(core, first, count):
+        @pl.loop(first, first + count)
+        def _(j):
+            there = pl.ds(pl.multiple_of(base + j * width, 128), width)
+            here = pl.ds(pl.multiple_of(j * width, 128), width)
+            change = jnp.dot(tall(s_all.at[core, :, :, :, pl.ds(0, panel)]), r_all[0, :, here], preferred_element_type=F32)
+            change = change + jnp.dot(
+                tall(s_all.at[core, :, :, :, pl.ds(panel, panel)]), r_all[1, :, here], preferred_element_type=F32)
+            fresh = (tall(v_all.at[core, :, :, :, here]).astype(F32) - change).astype(BF16)
+            v_all[core, :, :, :, here] = fresh.reshape(Q, 2, per, width)
+            for sender in range(2):
+                @pl.when(k == sender)
+                def _():
+                    for slot, flip in LEAVING[sender]:
+                        send(v_all.at[core, slot, sides[flip], :, here], out.at[prow, :, there],
+                             o_ssem.at[(slot * 2 + flip) * 2 + core],
+                             o_rsem.at[(turned(slot) * 2 + flip) * 2 + sender], place(slot, flip, core))
+                    if sender == core:
+                        pltpu.make_async_copy(
+                            v_all.at[core, 0, h, :, here], out.at[prow, :, there], o_own.at[0]).start()
+                    else:
+                        send(v_all.at[core, 0, h, :, here], out.at[prow, :, there], o_ssem.at[core],
+                             o_rsem.at[sender], place(0, 0, core))
+
+    s_out(0)
+    second_half(range(AHEAD[1], PIECES))
+    p_out(1)
+    s_shared(0)
+    results(0, 0, 3)
+    s_out(1)
+    results(0, 3, 3)
+    s_shared(1)
+    results(1, 0, 6)
 
     for slot in range(Q):
         if slot:
             arrived(piece(slot, 0), r_ssem.at[slot])
-            arrived(v_all.at[rows_at(slot), :], v_ssem.at[slot])
+        for number in (None, *range(PIECES)) if slot else ():
+            arrived(v_landing(slot, number), v_ssem.at[v_sem(slot, number)])
         for dx in (1, 3):
             arrived(piece(slot, 0), x_ssem.at[dx * Q + slot])
         for number in range(2):
@@ -245,13 +379,23 @@
     for d in OTHERS:
         arrived(g_own, gs_ssem.at[d])
         arrived(g_own, ga_ssem.at[d])
-        arrived(p_recv.at[0], ps_ssem.at[d])
         arrived(s_own, sa_ssem.at[d])
-        arrived(piece_rows, o_ssem.at[d])
-    for d in OTHERS:
-        across, far = at(d)
+
+    def ended(spot):
+        arrived(s_own, ps_ssem.at[spot])
+        arrived(piece_rows, o_ssem.at[spot])
+
+    def landed(slot, flip, core):
+        across, far = place(slot, flip, core)
         there = pl.ds(pl.multiple_of(lax.rem(far, Q) * chunk, 128), chunk)
-        arrived(out.at[across, :, there], o_rsem.at[d])
+        arrived(out.at[across, :, there], o_rsem.at[(slot * 2 + flip) * 2 + core])
+
+    ended(1 - k)
+    landed(0, 0, 1 - k)
+    for slot, flip in FAR:
+        for core in range(2):
+            ended((slot * 2 + flip) * 2 + core)
+            landed(slot, flip, core)
 
 
 def joined(width, pieces, out, held, line, in_sem, out_sem):
@@ -309,21 +453,22 @@
         ],
         out_specs=any_spec,
         scratch_shapes=[
-            pltpu.VMEM((rows, chunk * Q), BF16),
+            pltpu.VMEM((2, 2, per, chunk * Q), BF16),
             pltpu.VMEM((2, share, chunk * Q), BF16),
-            pltpu.VMEM((rows * Q, chunk), BF16),
+            pltpu.VMEM((2, Q, 2, per, chunk), BF16),
             pltpu.VMEM((2, panel, chunk), BF16),
-            pltpu.VMEM((rows * Q, 2 * panel), BF16),
+            pltpu.VMEM((rows * Q // 2, 2 * panel), F32),
+            pltpu.VMEM((2, Q, 2, per, 2 * panel), BF16),
             pltpu.VMEM((GROUP, per, 2 * panel), BF16),
             pltpu.VMEM((GROUP, part, panel), BF16),
             pltpu.VMEM((GROUP, part, panel), BF16),
             pltpu.VMEM((part, panel), BF16),
             pltpu.VMEM((GROUP, part, panel), BF16),
             pltpu.VMEM((per, 2 * panel), BF16),
-            pltpu.VMEM((rows * Q, 2 * panel), BF16),
+            pltpu.VMEM((2, Q, 2, per, 2 * panel), BF16),
             pltpu.VMEM((2, panel, panel), BF16),
             pltpu.VMEM((2, panel, panel), BF16),
-            dma((2,)), dma((2,)), dma((Q,)), dma(((X + 1) * Q,)), dma((X * Q,)), dma((Q,)), dma((Q,)),
+            dma((1 + R,)), dma((3,)), dma((Q,)), dma(((X + 1) * Q,)), dma((X * Q,)), dma((Q + Q * PIECES,)), dma((Q + Q * PIECES,)),
             dma((GROUP,)), dma((GROUP,)), dma((GROUP,)), dma((GROUP,)), dma((GROUP,)), dma((GROUP,)),
             dma((GROUP,)), dma((GROUP,)), dma((GROUP,)), dma((GROUP,)), dma((1,)),
         ],

time: 143 us -> 129 us (0.902)
  Pallas kernels: 143 us -> 129 us
    pallas_call x1, Pallas kernels: 139 us -> 125 us  [body(): pl.pallas_call(functools.partial(kernel, dims), grid=(1,), out_shape=jax....]
where the time goes in v5:
time: 129 us
  Pallas kernels  129 us (100%)
    pallas_call x1, Pallas kernels, body(): pl.pallas_call(functools.partial(kernel, dims), grid=(1,), out_shape=jax....  125 us
    pallas_call x1, Pallas kernels, body(): pl.pallas_call(functools.partial(joined, width), out_shape=jax.ShapeDtype...  3.48 us

profile of v5, /device:TPU:1, one launch (start us, length us, event | category | flops | bytes accessed | tf_op | source)
XLA Modules:
  0.0 128.8 jit_solution(3913828986015593615)
XLA Ops:
  0.0 125.3 %back_transform.1.pieces = bf16[4,16,30720]{2,1,0:T(8,128)(2,1)} custom-call(bf16[64,30016]{1,0:T(8,128)(2,1)} %v_tail.1, bf16[2,8,30016]{2,1,0:T(8,128)(2,1)} %r_tail.1, bf16[64,30016]{1,0:T(8,128)(2,1)} %v_tail.1, bf16[2,8,30016]{2,1,0:T(8,128)(2,1)} %r_tail.1, f32[2,256,256]{2,1,0:T(8,128)} %factor.1), custom_call_target="tpu_custom_call" | custom-call | tf_op jit(solution)/shard_map/back_transform/pallas_call | solution.py:444
  125.3 3.5 %joined.1 = bf16[16,120064]{1,0:T(8,128)(2,1)} custom-call(bf16[4,16,30720]{2,1,0:T(8,128)(2,1)} %back_transform.1.pieces), custom_call_target="tpu_custom_call" | custom-call | tf_op jit(solution)/shard_map/joined/pallas_call | solution.py:481

commit v6 on v5

--- a/solution.py
+++ b/solution.py
@@ -13,7 +13,7 @@
 ORDER = ((0, 0), (1, 0), (1, 1), (1, 3), (0, 2), (1, 2), (0, 1), (0, 3))
 SLOT = {pair: number for number, pair in enumerate(ORDER)}
 PAIRS = [(slot, flip) for slot in range(Q) for flip in range(2)]
-PIECES, AHEAD = 5, (2, 3, 4, 5)
+PIECES, AHEAD = 5, (2, 2, 3, 5)
 GOING = ((1, 2), (1, 0), (0, 2), (1, 1), (0, 3), (1, 3), (0, 1))
 
 
@@ -24,25 +24,6 @@
 
 OTHERS = sorted(range(1, GROUP), key=lambda d: -hops(d))
 
-TURNS = (
-    (
-        ((0, 1, 2),),
-        ((0, 1, 1), (0, 1, 3), (0, 0, 1), (0, 0, 3)),
-        ((1, 0, 1), (1, 1, 3)),
-        ((1, 0, 3), (1, 1, 1)),
-        ((1, 0, 2), (1, 1, 2), (1, 0, 0), (1, 1, 0)),
-        ((0, 1, 0), (0, 0, 2)),
-    ),
-    (
-        ((1, 0, 0), (1, 1, 0), (1, 0, 2), (1, 1, 2)),
-        ((1, 0, 1), (1, 1, 3)),
-        ((1, 0, 3), (1, 1, 1)),
-        ((0, 1, 2),),
-        ((0, 1, 0), (0, 0, 2)),
-        ((0, 1, 1), (0, 1, 3), (0, 0, 1), (0, 0, 3)),
-    ),
-)
-LEAVING = [[(SLOT[lo, dz], hi) for turn in turns for lo, hi, dz in turn] for turns in TURNS]
 FAR = sorted(PAIRS[1:], key=lambda pair: -hops(pair[0] * R + pair[1] * 2))
 BF16, F32 = jnp.bfloat16, jnp.float32
 NT = (((1,), (1,)), ((), ()))
@@ -67,9 +48,9 @@
 
 def kernel(
     dims,
-    v_hbm, r_hbm, v_tail, r_tail, factor,
+    v_hbm, r_hbm, f_hbm,
     out,
-    v_loc, r_loc, v_all, r_all, p_sum, p_send, p_recv, g_send, g_recv, g_own, g_all, s_own, s_all, f_high, f_low,
+    v_loc, r_loc, v_all, r_all, p_sum, p_send, p_recv, g_send, g_recv, g_own, g_all, s_own, s_all, v_tail, r_tail, factor, f_high, f_low,
     ld_sem, own_sem, r_ssem, r_rsem, x_ssem, v_ssem, v_rsem,
     gs_ssem, gs_rsem, ga_ssem, ga_rsem, ps_ssem, ps_rsem, sa_ssem, sa_rsem, o_ssem, o_rsem, o_own,
 ):
@@ -101,6 +82,12 @@
     def arrived(ref, sem):
         pltpu.make_async_copy(ref, ref, sem).wait()
 
+    barrier = pltpu.get_barrier_semaphore()
+    for d in OTHERS:
+        pl.semaphore_signal(barrier, inc=1, device_id=at(d), device_id_type=pl.DeviceIdType.MESH)
+    for dx in (1, 3):
+        pl.semaphore_signal(barrier, inc=1, device_id=at(0, dx), device_id_type=pl.DeviceIdType.MESH)
+
     load_r = pltpu.make_async_copy(r_hbm.at[:, :, pl.ds(0, whole)], r_loc.at[:, :, pl.ds(0, whole)], ld_sem.at[0])
     load_v = [
         pltpu.make_async_copy(
@@ -110,23 +97,24 @@
     load_r.start()
     for load in load_v:
         load.start()
-
-    barrier = pltpu.get_barrier_semaphore()
-    for d in OTHERS:
-        pl.semaphore_signal(barrier, inc=1, device_id=at(d), device_id_type=pl.DeviceIdType.MESH)
-    for dx in (1, 3):
-        pl.semaphore_signal(barrier, inc=1, device_id=at(0, dx), device_id_type=pl.DeviceIdType.MESH)
+    load_f = pltpu.make_async_copy(f_hbm, factor, ld_sem.at[1 + R])
+    load_f.start()
+    tails = [
+        pltpu.make_async_copy(v_hbm.at[:, pl.ds(whole, valid)], v_tail, ld_sem.at[2 + R]),
+        pltpu.make_async_copy(r_hbm.at[:, :, pl.ds(whole, valid)], r_tail, ld_sem.at[3 + R]),
+    ]
+    for load in tails:
+        load.start()
 
     edge = v_loc.shape[3] - whole
-    lane = lax.broadcasted_iota(jnp.int32, (rows, 128), 1)
-    tail = jnp.where(lane < valid, v_tail[...].astype(F32), 0.0).astype(BF16)
+    for load in tails:
+        load.wait()
     for r in range(R):
         v_loc[r // 2, r % 2, :, whole:] = jnp.zeros((per, edge), BF16)
-        v_loc[r // 2, r % 2, :, whole:whole + 128] = tail[r * per:(r + 1) * per]
-    lane8 = lax.broadcasted_iota(jnp.int32, (share, 128), 1)
+        v_loc[r // 2, r % 2, :, whole:whole + valid] = v_tail[r * per:(r + 1) * per, :]
     for p in range(2):
         r_loc[p, :, whole:] = jnp.zeros((share, edge), BF16)
-        r_loc[p, :, whole:whole + 128] = jnp.where(lane8 < valid, r_tail[p].astype(F32), 0.0).astype(BF16)
+        r_loc[p, :, whole:whole + valid] = r_tail[p]
 
     pl.semaphore_wait(barrier, GROUP - 1 + 2)
 
@@ -203,6 +191,7 @@
         if slot >= lag:
             relay(slot - lag)
 
+    load_f.wait()
     f_high[...], f_low[...] = halves(factor[...])
     for slot in range(Q):
         for number in range(2):
@@ -341,19 +330,19 @@
                 tall(s_all.at[core, :, :, :, pl.ds(panel, panel)]), r_all[1, :, here], preferred_element_type=F32)
             fresh = (tall(v_all.at[core, :, :, :, here]).astype(F32) - change).astype(BF16)
             v_all[core, :, :, :, here] = fresh.reshape(Q, 2, per, width)
-            for sender in range(2):
-                @pl.when(k == sender)
-                def _():
-                    for slot, flip in LEAVING[sender]:
-                        send(v_all.at[core, slot, sides[flip], :, here], out.at[prow, :, there],
-                             o_ssem.at[(slot * 2 + flip) * 2 + core],
-                             o_rsem.at[(turned(slot) * 2 + flip) * 2 + sender], place(slot, flip, core))
-                    if sender == core:
-                        pltpu.make_async_copy(
-                            v_all.at[core, 0, h, :, here], out.at[prow, :, there], o_own.at[0]).start()
-                    else:
-                        send(v_all.at[core, 0, h, :, here], out.at[prow, :, there], o_ssem.at[core],
-                             o_rsem.at[sender], place(0, 0, core))
+            for slot, flip in FAR:
+                send(v_all.at[core, slot, sides[flip], :, here], out.at[prow, :, there],
+                     o_ssem.at[(slot * 2 + flip) * 2 + core], o_rsem.at[(turned(slot) * 2 + flip) * 2 + k],
+                     place(slot, flip, core))
+
+            @pl.when(k == core)
+            def _():
+                pltpu.make_async_copy(v_all.at[core, 0, h, :, here], out.at[prow, :, there], o_own.at[0]).start()
+
+            @pl.when(k != core)
+            def _():
+                send(v_all.at[core, 0, h, :, here], out.at[prow, :, there], o_ssem.at[core], o_rsem.at[k],
+                     place(0, 0, core))
 
     s_out(0)
     second_half(range(AHEAD[1], PIECES))
@@ -398,14 +387,10 @@
             landed(slot, flip, core)
 
 
-def joined(width, pieces, out, held, line, in_sem, out_sem):
-    loads = [pltpu.make_async_copy(pieces.at[r], held.at[r], in_sem.at[r]) for r in range(R)]
-    for load in loads:
-        load.start()
+def joined(width, held, out, line, out_sem):
     stores = []
     rows = held.shape[1]
-    for r in range(R):
-        loads[r].wait()
+    for r in sorted(range(R), key=lambda r: r * width % 128):
         first, shift = r * width // 128 * 128, r * width % 128
         end = (r + 1) * width // 128 * 128
         if shift == 0:
@@ -443,15 +428,12 @@
     part = panel // GROUP
     gathered = pl.pallas_call(
         functools.partial(kernel, dims),
-        grid=(1,),
-        out_shape=jax.ShapeDtypeStruct((R, per, chunk * Q), BF16),
+        out_shape=pltpu.VMEM((R, per, chunk * Q), BF16),
         in_specs=[
             any_spec, any_spec,
-            pl.BlockSpec((rows, 128), lambda i: (0, tiles - 1)),
-            pl.BlockSpec((2, share, 128), lambda i: (0, 0, tiles - 1)),
-            pl.BlockSpec((2, panel, panel), lambda i: (0, 0, 0)),
+            any_spec,
         ],
-        out_specs=any_spec,
+        out_specs=pl.BlockSpec(memory_space=pltpu.VMEM),
         scratch_shapes=[
             pltpu.VMEM((2, 2, per, chunk * Q), BF16),
             pltpu.VMEM((2, share, chunk * Q), BF16),
@@ -466,27 +448,28 @@
             pltpu.VMEM((GROUP, part, panel), BF16),
             pltpu.VMEM((per, 2 * panel), BF16),
             pltpu.VMEM((2, Q, 2, per, 2 * panel), BF16),
+            pltpu.VMEM((rows, width - whole), BF16),
+            pltpu.VMEM((2, share, width - whole), BF16),
+            pltpu.VMEM((2, panel, panel), F32),
             pltpu.VMEM((2, panel, panel), BF16),
             pltpu.VMEM((2, panel, panel), BF16),
-            dma((1 + R,)), dma((3,)), dma((Q,)), dma(((X + 1) * Q,)), dma((X * Q,)), dma((Q + Q * PIECES,)), dma((Q + Q * PIECES,)),
+            dma((4 + R,)), dma((3,)), dma((Q,)), dma(((X + 1) * Q,)), dma((X * Q,)), dma((Q + Q * PIECES,)), dma((Q + Q * PIECES,)),
             dma((GROUP,)), dma((GROUP,)), dma((GROUP,)), dma((GROUP,)), dma((GROUP,)), dma((GROUP,)),
             dma((GROUP,)), dma((GROUP,)), dma((GROUP,)), dma((GROUP,)), dma((1,)),
         ],
         compiler_params=pltpu.CompilerParams(
-            collective_id=0, has_side_effects=True, vmem_limit_bytes=61 * 1024 * 1024
+            collective_id=0, has_side_effects=True, vmem_limit_bytes=62700000
         ),
         name="back_transform",
-    )(vectors, reflectors, vectors, reflectors, panel_factor)
+    )(vectors, reflectors, panel_factor)
     line = R * width // 128 * 128 - (R - 1) * width // 128 * 128
     rows_out = pl.pallas_call(
         functools.partial(joined, width),
         out_shape=jax.ShapeDtypeStruct((per, R * width), BF16),
-        in_specs=[any_spec],
+        in_specs=[pl.BlockSpec(memory_space=pltpu.VMEM)],
         out_specs=any_spec,
-        scratch_shapes=[
-            pltpu.VMEM((R, per, chunk * Q), BF16), pltpu.VMEM((2, per, line), BF16), dma((R,)), dma((R,)),
-        ],
-        compiler_params=pltpu.CompilerParams(vmem_limit_bytes=61 * 1024 * 1024),
+        scratch_shapes=[pltpu.VMEM((2, per, line), BF16), dma((R,))],
+        compiler_params=pltpu.CompilerParams(vmem_limit_bytes=16 * 1024 * 1024),
         name="joined",
     )(gathered)
     return rows_out[None]

time: 129 us -> 125 us (0.969)
  Pallas kernels: 129 us -> 125 us
    pallas_call x1, Pallas kernels: 125 us -> 123 us  [body(): pl.pallas_call(functools.partial(kernel, dims), out_shape=pltpu.VMEM((R,...]
    pallas_call x1, Pallas kernels: 3.48 us -> 1.94 us  [body(): pl.pallas_call(functools.partial(joined, width), out_shape=jax.ShapeDtype...]
where the time goes in v6:
time: 125 us
  Pallas kernels  125 us (100%)
    pallas_call x1, Pallas kernels, body(): pl.pallas_call(functools.partial(kernel, dims), out_shape=pltpu.VMEM((R,...  123 us

profile of v6, /device:TPU:1, one launch (start us, length us, event | category | flops | bytes accessed | tf_op | source)
XLA Modules:
  0.0 125.1 jit_solution(2754915655829754994)
XLA Ops:
  0.0 123.2 %back_transform.1.held = bf16[4,16,30720]{2,1,0:T(8,128)(2,1)S(1)} custom-call(bf16[64,30016]{1,0:T(8,128)(2,1)} %v_hbm.1, bf16[2,8,30016]{2,1,0:T(8,128)(2,1)} %r_hbm.1, f32[2,256,256]{2,1,0:T(8,128)} %f_hbm.1), custom_call_target="tpu_custom_call" | custom-call | tf_op jit(solution)/shard_map/back_transform/pallas_call | solution.py:429
  123.2 1.9 %joined.1 = bf16[16,120064]{1,0:T(8,128)(2,1)} custom-call(bf16[4,16,30720]{2,1,0:T(8,128)(2,1)S(1)} %back_transform.1.held), custom_call_target="tpu_custom_call" | custom-call | tf_op jit(solution)/shard_map/joined/pallas_call | solution.py:466

commit v7 on v6

--- a/solution.py
+++ b/solution.py
@@ -14,7 +14,7 @@
 SLOT = {pair: number for number, pair in enumerate(ORDER)}
 PAIRS = [(slot, flip) for slot in range(Q) for flip in range(2)]
 PIECES, AHEAD = 5, (2, 2, 3, 5)
-GOING = ((1, 2), (1, 0), (0, 2), (1, 1), (0, 3), (1, 3), (0, 1))
+GOING = ((0, 1), (0, 3), (1, 1), (1, 3), (1, 0), (0, 2), (1, 2))
 
 
 def hops(d):
@@ -54,7 +54,7 @@
     ld_sem, own_sem, r_ssem, r_rsem, x_ssem, v_ssem, v_rsem,
     gs_ssem, gs_rsem, ga_ssem, ga_rsem, ps_ssem, ps_rsem, sa_ssem, sa_rsem, o_ssem, o_rsem, o_own,
 ):
-    rows, panel, whole, valid, chunk, step = dims
+    rows, panel, whole, valid, chunk, slim, extras, step = dims
     per = rows // R
     share = panel // (X * Q)
     half = chunk // 2
@@ -81,6 +81,29 @@
 
     def arrived(ref, sem):
         pltpu.make_async_copy(ref, ref, sem).wait()
+
+    def first_of(q):
+        return (q * (slim // 128) + sum((q + (Q - 1 - e)) // Q for e in extras)) * 128
+
+    def wide(q):
+        return sum((q + (Q - e)) // Q - (q + (Q - 1 - e)) // Q for e in extras) == 1
+
+    def place_q(slot):
+        return yls[ORDER[slot][0]] * Z + zs[ORDER[slot][1]]
+
+    def either(q, action, most=chunk):
+        @pl.when(wide(q))
+        def _():
+            action(most)
+
+        @pl.when(jnp.logical_not(wide(q)))
+        def _():
+            action(most - 128)
+
+    @pl.when(jnp.logical_not(wide(place_q(0))))
+    def _():
+        v_all[:, :, :, :, slim:] = jnp.zeros((2, Q, 2, per, chunk - slim), BF16)
+        r_all[:, :, slim:] = jnp.zeros((2, panel, chunk - slim), BF16)
 
     barrier = pltpu.get_barrier_semaphore()
     for d in OTHERS:
@@ -120,30 +143,36 @@
 
     mine = pl.ds(pl.multiple_of(pcol * share, share), share)
 
-    def columns(slot):
-        q = lax.rem(at(slot * R)[1], Q)
-        return pl.ds(pl.multiple_of(q * chunk, 128), chunk)
+    def columns(slot, count, skip=0):
+        return pl.ds(pl.multiple_of(first_of(place_q(slot)) + skip, 128), count)
 
     load_r.wait()
-    own_r = pltpu.make_async_copy(r_loc.at[:, :, columns(0)], r_all.at[:, mine, :], own_sem.at[0])
-    own_r.start()
+    def r_mine(count):
+        return r_all.at[:, mine, pl.ds(0, count)]
+
+    either(place_q(0), lambda n: pltpu.make_async_copy(r_loc.at[:, :, columns(0, n)], r_mine(n), own_sem.at[0]).start())
     for slot in range(1, Q):
         d = mirror(slot * R)
-        send(r_loc.at[:, :, columns(d // R)], r_all.at[:, mine, :], r_ssem.at[slot], r_rsem.at[slot], at(d))
+        either(place_q(d // R), lambda n: send(
+            r_loc.at[:, :, columns(d // R, n)], r_mine(n), r_ssem.at[slot], r_rsem.at[slot], at(d)))
     part_width = chunk // PIECES
 
     def v_sem(slot, number):
         return slot if number is None else Q + slot * PIECES + number
 
-    def v_landing(slot, number=None):
+    def v_landing(slot, number, count):
+        return v_all.at[0 if number is None else 1, slot, :, :, pl.ds((number or 0) * part_width, count)]
+
+    def v_source(slot, number, count):
+        return v_loc.at[:, 0 if number is None else 1, :, columns(slot, count, (number or 0) * part_width)]
+
+    def v_each(q, number, action):
         if number is None:
-            return v_all.at[0, slot]
-        return v_all.at[1, slot, :, :, pl.ds(number * part_width, part_width)]
-
-    def v_source(slot, number):
-        first = lax.rem(at(slot * R)[1], Q) * chunk + (number or 0) * part_width
-        width = chunk if number is None else part_width
-        return v_loc.at[:, 0 if number is None else 1, :, pl.ds(pl.multiple_of(first, 128), width)]
+            either(q, action)
+        elif number == PIECES - 1:
+            either(q, action, part_width)
+        else:
+            action(part_width)
 
     def v_out(numbers):
         for number in numbers:
@@ -151,18 +180,30 @@
                 d = SLOT[pair] * R
                 slot = mirror(d) // R
                 sem = v_sem(slot, number)
-                send(v_source(d // R, number), v_landing(slot, number), v_ssem.at[sem], v_rsem.at[sem], at(d))
+                v_each(place_q(d // R), number, lambda n: send(
+                    v_source(d // R, number, n), v_landing(slot, number, n), v_ssem.at[sem], v_rsem.at[sem], at(d)))
+
+    def v_arrived(slot, number):
+        sem = v_rsem.at[v_sem(slot, number)]
+        v_each(place_q(0), number, lambda n: arrived(v_landing(slot, number, n), sem))
+
+    def own_copy(core):
+        def start(n):
+            pltpu.make_async_copy(
+                v_loc.at[:, core, :, columns(0, n)], v_all.at[core, 0, :, :, pl.ds(0, n)], own_sem.at[1 + core]).start()
+        either(place_q(0), start)
+
+    def own_copied(core):
+        either(place_q(0), lambda n: arrived(v_all.at[core, 0, :, :, pl.ds(0, n)], own_sem.at[1 + core]))
 
     load_v[0].wait()
     load_v[1].wait()
     v_out([None])
-    own_first = pltpu.make_async_copy(v_source(0, None), v_landing(0), own_sem.at[1])
-    own_first.start()
+    own_copy(0)
     load_v[2].wait()
     load_v[3].wait()
     v_out(range(AHEAD[0]))
-    own_second = pltpu.make_async_copy(v_loc.at[:, 1, :, columns(0)], v_all.at[1, 0], own_sem.at[2])
-    own_second.start()
+    own_copy(1)
 
     def piece(slot, dx, cols=None):
         source = pl.ds(pl.multiple_of(at(slot * R, dx)[1] * share, share), share)
@@ -171,10 +212,8 @@
     parts = (pl.ds(0, half), pl.ds(half, half))
 
     def spread(slot):
-        if slot == 0:
-            own_r.wait()
-        else:
-            arrived(piece(slot, 0), r_rsem.at[slot])
+        came = r_rsem.at[slot] if slot else own_sem.at[0]
+        either(place_q(0), lambda n: arrived(piece(slot, 0, pl.ds(0, n)), came))
         for dx in (1, 3):
             send(piece(slot, 0), piece(slot, 0), x_ssem.at[dx * Q + slot], r_rsem.at[(4 - dx) * Q + slot], at(0, dx))
 
@@ -241,8 +280,8 @@
             p_recv[k] = p_send[core, 0, h]
 
     for slot in range(1, Q):
-        arrived(v_landing(slot), v_rsem.at[slot])
-    own_first.wait()
+        v_arrived(slot, None)
+    own_copied(0)
     for p in range(2):
         total = summed(lambda cols: tall(v_all.at[0, :, :, :, cols]), lambda cols: r_all[p, :, cols], 2 * Q * per)
         p_send[0, :, :, :, p * panel:(p + 1) * panel] = total.astype(BF16).reshape(Q, 2, per, panel)
@@ -260,7 +299,7 @@
     def second_half(numbers):
         for number in numbers:
             for slot in range(1, Q):
-                arrived(v_landing(slot, number), v_rsem.at[v_sem(slot, number)])
+                v_arrived(slot, number)
             cols = pl.ds(number * part_width, part_width)
             for p in range(2):
                 here = slice(p * panel, (p + 1) * panel)
@@ -273,7 +312,7 @@
                 else:
                     p_send[1, :, :, :, here] = total.astype(BF16).reshape(Q, 2, per, panel)
 
-    own_second.wait()
+    own_copied(1)
     second_half(range(AHEAD[1]))
 
     def s_place(core, slot, flip):
@@ -317,19 +356,21 @@
             for slot, flip in FAR + [(0, 0)]:
                 arrived(s_place(core, slot, flip), sa_rsem.at[(slot * 2 + flip) * 2 + core])
 
-    base = lax.rem(pcol, Q) * chunk
+    base = first_of(place_q(0))
     width = chunk // 6
 
-    def results(core, first, count):
-        @pl.loop(first, first + count)
-        def _(j):
-            there = pl.ds(pl.multiple_of(base + j * width, 128), width)
+    def results(core, first, stop):
+        def update(j):
             here = pl.ds(pl.multiple_of(j * width, 128), width)
             change = jnp.dot(tall(s_all.at[core, :, :, :, pl.ds(0, panel)]), r_all[0, :, here], preferred_element_type=F32)
             change = change + jnp.dot(
                 tall(s_all.at[core, :, :, :, pl.ds(panel, panel)]), r_all[1, :, here], preferred_element_type=F32)
             fresh = (tall(v_all.at[core, :, :, :, here]).astype(F32) - change).astype(BF16)
             v_all[core, :, :, :, here] = fresh.reshape(Q, 2, per, width)
+
+        def leave(j, count):
+            there = pl.ds(pl.multiple_of(base + j * width, 128), count)
+            here = pl.ds(pl.multiple_of(j * width, 128), count)
             for slot, flip in FAR:
                 send(v_all.at[core, slot, sides[flip], :, here], out.at[prow, :, there],
                      o_ssem.at[(slot * 2 + flip) * 2 + core], o_rsem.at[(turned(slot) * 2 + flip) * 2 + k],
@@ -343,6 +384,16 @@
             def _():
                 send(v_all.at[core, 0, h, :, here], out.at[prow, :, there], o_ssem.at[core], o_rsem.at[k],
                      place(0, 0, core))
+
+        last = chunk // width - 1
+
+        @pl.loop(first, min(stop, last))
+        def _(j):
+            update(j)
+            leave(j, width)
+        if stop > last:
+            update(last)
+            either(place_q(0), lambda n: leave(last, n), width)
 
     s_out(0)
     second_half(range(AHEAD[1], PIECES))
@@ -350,21 +401,25 @@
     s_shared(0)
     results(0, 0, 3)
     s_out(1)
-    results(0, 3, 3)
+    results(0, 3, 6)
     s_shared(1)
     results(1, 0, 6)
 
     for slot in range(Q):
         if slot:
-            arrived(piece(slot, 0), r_ssem.at[slot])
-        for number in (None, *range(PIECES)) if slot else ():
-            arrived(v_landing(slot, number), v_ssem.at[v_sem(slot, number)])
+            q = place_q(turned(slot))
+            either(q, lambda n: arrived(piece(slot, 0, pl.ds(0, n)), r_ssem.at[slot]))
+            for number in (None, *range(PIECES)):
+                sem = v_ssem.at[v_sem(slot, number)]
+                v_each(q, number, lambda n: arrived(v_landing(slot, number, n), sem))
         for dx in (1, 3):
             arrived(piece(slot, 0), x_ssem.at[dx * Q + slot])
         for number in range(2):
             arrived(piece(slot, 0, parts[number]), x_ssem.at[2 * number * Q + slot])
-    piece_rows = out.at[0, :, pl.ds(0, chunk)]
-    arrived(piece_rows, o_own.at[0])
+    def out_rows(n):
+        return out.at[0, :, pl.ds(0, n)]
+
+    either(place_q(0), lambda n: arrived(out_rows(n), o_own.at[0]))
     for d in OTHERS:
         arrived(g_own, gs_ssem.at[d])
         arrived(g_own, ga_ssem.at[d])
@@ -372,12 +427,15 @@
 
     def ended(spot):
         arrived(s_own, ps_ssem.at[spot])
-        arrived(piece_rows, o_ssem.at[spot])
+        either(place_q(0), lambda n: arrived(out_rows(n), o_ssem.at[spot]))
 
     def landed(slot, flip, core):
-        across, far = place(slot, flip, core)
-        there = pl.ds(pl.multiple_of(lax.rem(far, Q) * chunk, 128), chunk)
-        arrived(out.at[across, :, there], o_rsem.at[(slot * 2 + flip) * 2 + core])
+        q = place_q(slot)
+
+        def wait(n):
+            there = pl.ds(pl.multiple_of(first_of(q), 128), n)
+            arrived(out.at[place(slot, flip, core)[0], :, there], o_rsem.at[(slot * 2 + flip) * 2 + core])
+        either(q, wait)
 
     ended(1 - k)
     landed(0, 0, 1 - k)
@@ -421,22 +479,24 @@
     tiles = pl.cdiv(width, 128)
     chunk = pl.cdiv(tiles, Q) * 128
     whole = (tiles - 1) * 128
-    dims = (rows, panel, whole, width - whole, chunk, chunk // 3)
+    slim = tiles // Q * 128
+    extras = tuple(number * Q // (tiles % Q) for number in range(tiles % Q))
+    dims = (rows, panel, whole, width - whole, chunk, slim, extras, chunk // 3)
     per = rows // R
     any_spec = pl.BlockSpec(memory_space=pl.ANY)
     dma = pltpu.SemaphoreType.DMA
     part = panel // GROUP
     gathered = pl.pallas_call(
         functools.partial(kernel, dims),
-        out_shape=pltpu.VMEM((R, per, chunk * Q), BF16),
+        out_shape=pltpu.VMEM((R, per, tiles * 128), BF16),
         in_specs=[
             any_spec, any_spec,
             any_spec,
         ],
         out_specs=pl.BlockSpec(memory_space=pltpu.VMEM),
         scratch_shapes=[
-            pltpu.VMEM((2, 2, per, chunk * Q), BF16),
-            pltpu.VMEM((2, share, chunk * Q), BF16),
+            pltpu.VMEM((2, 2, per, tiles * 128), BF16),
+            pltpu.VMEM((2, share, tiles * 128), BF16),
             pltpu.VMEM((2, Q, 2, per, chunk), BF16),
             pltpu.VMEM((2, panel, chunk), BF16),
             pltpu.VMEM((rows * Q // 2, 2 * panel), F32),

time: 125 us -> 124 us (level)
  no operation moved by 1% of the time
where the time goes in v7:
time: 124 us
  Pallas kernels  124 us (100%)
    pallas_call x1, Pallas kernels, body(): pl.pallas_call(functools.partial(kernel, dims), out_shape=pltpu.VMEM((R,...  122 us

profile of v7, /device:TPU:1, one launch (start us, length us, event | category | flops | bytes accessed | tf_op | source)
XLA Modules:
  0.0 124.0 jit_solution(8954847586303986544)
XLA Ops:
  0.0 122.1 %back_transform.1.held = bf16[4,16,30080]{2,1,0:T(8,128)(2,1)S(1)} custom-call(bf16[64,30016]{1,0:T(8,128)(2,1)} %v_hbm.1, bf16[2,8,30016]{2,1,0:T(8,128)(2,1)} %r_hbm.1, f32[2,256,256]{2,1,0:T(8,128)} %f_hbm.1), custom_call_target="tpu_custom_call" | custom-call | tf_op jit(solution)/shard_map/back_transform/pallas_call | solution.py:489
  122.1 1.9 %joined.1 = bf16[16,120064]{1,0:T(8,128)(2,1)} custom-call(bf16[4,16,30080]{2,1,0:T(8,128)(2,1)S(1)} %back_transform.1.held), custom_call_target="tpu_custom_call" | custom-call | tf_op jit(solution)/shard_map/joined/pallas_call | solution.py:526

commit v8 on v7

--- a/solution.py
+++ b/solution.py
@@ -13,7 +13,7 @@
 ORDER = ((0, 0), (1, 0), (1, 1), (1, 3), (0, 2), (1, 2), (0, 1), (0, 3))
 SLOT = {pair: number for number, pair in enumerate(ORDER)}
 PAIRS = [(slot, flip) for slot in range(Q) for flip in range(2)]
-PIECES, AHEAD = 5, (2, 2, 3, 5)
+PIECES, AHEAD = 5, (2, 3, 4, 5)
 GOING = ((0, 1), (0, 3), (1, 1), (1, 3), (1, 0), (0, 2), (1, 2))
 
 
@@ -25,6 +25,7 @@
 OTHERS = sorted(range(1, GROUP), key=lambda d: -hops(d))
 
 FAR = sorted(PAIRS[1:], key=lambda pair: -hops(pair[0] * R + pair[1] * 2))
+DISTANT = sorted(range(1, Q), key=lambda slot: -hops(slot * R))
 BF16, F32 = jnp.bfloat16, jnp.float32
 NT = (((1,), (1,)), ((), ()))
 
@@ -50,9 +51,9 @@
     dims,
     v_hbm, r_hbm, f_hbm,
     out,
-    v_loc, r_loc, v_all, r_all, p_sum, p_send, p_recv, g_send, g_recv, g_own, g_all, s_own, s_all, v_tail, r_tail, factor, f_high, f_low,
+    v_loc, r_loc, v_all, r_all, p_sum, p_send, p_swap, p_recv, g_send, g_recv, g_own, g_all, s_own, s_all, v_tail, r_tail, factor, f_high, f_low,
     ld_sem, own_sem, r_ssem, r_rsem, x_ssem, v_ssem, v_rsem,
-    gs_ssem, gs_rsem, ga_ssem, ga_rsem, ps_ssem, ps_rsem, sa_ssem, sa_rsem, o_ssem, o_rsem, o_own,
+    pw_ssem, pw_rsem, gs_ssem, gs_rsem, ga_ssem, ga_rsem, ps_ssem, ps_rsem, sa_ssem, sa_rsem, o_ssem, o_rsem, o_own,
 ):
     rows, panel, whole, valid, chunk, slim, extras, step = dims
     per = rows // R
@@ -266,18 +267,29 @@
         value = ref[...]
         return value.reshape(2 * Q * per, value.shape[-1])
 
+    step_y = lax.rem(h + k, 2)
+
     def p_out(core):
-        for slot, flip in FAR:
-            send(p_send.at[core, slot, sides[flip]], p_recv.at[(turned(slot) * 2 + flip) * 2 + k],
-                 ps_ssem.at[(slot * 2 + flip) * 2 + core], ps_rsem.at[(turned(slot) * 2 + flip) * 2 + k], place(slot, flip, core))
-
-        @pl.when(k != core)
-        def _():
-            send(p_send.at[core, 0, h], p_recv.at[k], ps_ssem.at[core], ps_rsem.at[k], place(0, 0, core))
-
-        @pl.when(k == core)
-        def _():
-            p_recv[k] = p_send[core, 0, h]
+        send(p_send.at[core, :, 1 - k], p_swap.at[core], pw_ssem.at[core], pw_rsem.at[core], place(0, 0, 1 - k))
+        arrived(p_swap.at[core], pw_rsem.at[core])
+        p_send[core, :, k] = (p_send[core, :, k].astype(F32) + p_swap[core].astype(F32)).astype(BF16)
+
+        def p_to(slot):
+            spot = turned(slot) * 2 + step_y
+            send(p_send.at[core, slot, k], p_recv.at[spot], ps_ssem.at[slot * 2 + core], ps_rsem.at[spot],
+                 (k * 2 + core, at(slot * R)[1]))
+
+        for slot in DISTANT:
+            p_to(slot)
+        here = jnp.logical_and(h == core, k == core)
+
+        @pl.when(jnp.logical_not(here))
+        def _():
+            p_to(0)
+
+        @pl.when(here)
+        def _():
+            p_recv[0] = p_send[core, 0, core]
 
     for slot in range(1, Q):
         v_arrived(slot, None)
@@ -321,11 +333,12 @@
     def s_out(core):
         @pl.when(k == core)
         def _():
-            for slot, flip in FAR:
-                for sender in range(2):
-                    spot = (slot * 2 + flip) * 2 + sender
-                    arrived(p_recv.at[spot], ps_rsem.at[spot])
-            arrived(p_recv.at[1 - k], ps_rsem.at[1 - k])
+            for spot in range(1, 2 * Q):
+                arrived(p_recv.at[spot], ps_rsem.at[spot])
+
+            @pl.when(h != core)
+            def _():
+                arrived(p_recv.at[0], ps_rsem.at[0])
             product = jnp.sum(p_recv[...].astype(F32), axis=0)
             first = times(product[:, :panel], f_high[0], f_low[0]).astype(BF16)
             second = times(product[:, panel:], f_high[1], f_low[1])
@@ -426,7 +439,6 @@
         arrived(s_own, sa_ssem.at[d])
 
     def ended(spot):
-        arrived(s_own, ps_ssem.at[spot])
         either(place_q(0), lambda n: arrived(out_rows(n), o_ssem.at[spot]))
 
     def landed(slot, flip, core):
@@ -436,6 +448,15 @@
             there = pl.ds(pl.multiple_of(first_of(q), 128), n)
             arrived(out.at[place(slot, flip, core)[0], :, there], o_rsem.at[(slot * 2 + flip) * 2 + core])
         either(q, wait)
+
+    for core in range(2):
+        arrived(p_swap.at[core], pw_ssem.at[core])
+        for slot in DISTANT:
+            arrived(s_own, ps_ssem.at[slot * 2 + core])
+
+        @pl.when(jnp.logical_not(jnp.logical_and(h == core, k == core)))
+        def _():
+            arrived(s_own, ps_ssem.at[core])
 
     ended(1 - k)
     landed(0, 0, 1 - k)
@@ -501,7 +522,8 @@
             pltpu.VMEM((2, panel, chunk), BF16),
             pltpu.VMEM((rows * Q // 2, 2 * panel), F32),
             pltpu.VMEM((2, Q, 2, per, 2 * panel), BF16),
-            pltpu.VMEM((GROUP, per, 2 * panel), BF16),
+            pltpu.VMEM((2, Q, per, 2 * panel), BF16),
+            pltpu.VMEM((2 * Q, per, 2 * panel), BF16),
             pltpu.VMEM((GROUP, part, panel), BF16),
             pltpu.VMEM((GROUP, part, panel), BF16),
             pltpu.VMEM((part, panel), BF16),
@@ -514,7 +536,8 @@
             pltpu.VMEM((2, panel, panel), BF16),
             pltpu.VMEM((2, panel, panel), BF16),
             dma((4 + R,)), dma((3,)), dma((Q,)), dma(((X + 1) * Q,)), dma((X * Q,)), dma((Q + Q * PIECES,)), dma((Q + Q * PIECES,)),
-            dma((GROUP,)), dma((GROUP,)), dma((GROUP,)), dma((GROUP,)), dma((GROUP,)), dma((GROUP,)),
+            dma((2,)), dma((2,)),
+            dma((GROUP,)), dma((GROUP,)), dma((GROUP,)), dma((GROUP,)), dma((2 * Q,)), dma((2 * Q,)),
             dma((GROUP,)), dma((GROUP,)), dma((GROUP,)), dma((GROUP,)), dma((1,)),
         ],
         compiler_params=pltpu.CompilerParams(

time: 124 us -> 123 us (level)
    pallas_call x1, Pallas kernels: 122 us -> 121 us  [body(): pl.pallas_call(functools.partial(kernel, dims), out_shape=pltpu.VMEM((R,...]
where the time goes in v8:
time: 123 us
  Pallas kernels  123 us (100%)
    pallas_call x1, Pallas kernels, body(): pl.pallas_call(functools.partial(kernel, dims), out_shape=pltpu.VMEM((R,...  121 us

profile of v8, /device:TPU:1, one launch (start us, length us, event | category | flops | bytes accessed | tf_op | source)
XLA Modules:
  0.0 122.8 jit_solution(17661043754366488933)
XLA Ops:
  0.0 120.8 %back_transform.1.held = bf16[4,16,30080]{2,1,0:T(8,128)(2,1)S(1)} custom-call(bf16[64,30016]{1,0:T(8,128)(2,1)} %v_hbm.1, bf16[2,8,30016]{2,1,0:T(8,128)(2,1)} %r_hbm.1, f32[2,256,256]{2,1,0:T(8,128)} %f_hbm.1), custom_call_target="tpu_custom_call" | custom-call | tf_op jit(solution)/shard_map/back_transform/pallas_call | solution.py:510
  120.8 1.9 %joined.1 = bf16[16,120064]{1,0:T(8,128)(2,1)} custom-call(bf16[4,16,30080]{2,1,0:T(8,128)(2,1)S(1)} %back_transform.1.held), custom_call_target="tpu_custom_call" | custom-call | tf_op jit(solution)/shard_map/joined/pallas_call | solution.py:549

commit v9 on v8

--- a/solution.py
+++ b/solution.py
@@ -412,9 +412,9 @@
     second_half(range(AHEAD[1], PIECES))
     p_out(1)
     s_shared(0)
-    results(0, 0, 3)
+    results(0, 0, 2)
     s_out(1)
-    results(0, 3, 6)
+    results(0, 2, 6)
     s_shared(1)
     results(1, 0, 6)
 

time: 123 us -> 123 us (level)
  no operation moved by 1% of the time
where the time goes in v9:
time: 123 us
  Pallas kernels  123 us (100%)
    pallas_call x1, Pallas kernels, body(): pl.pallas_call(functools.partial(kernel, dims), out_shape=pltpu.VMEM((R,...  121 us

profile of v9, /device:TPU:1, one launch (start us, length us, event | category | flops | bytes accessed | tf_op | source)
XLA Modules:
  0.0 122.8 jit_solution(9615925904348885980)
XLA Ops:
  0.0 120.8 %back_transform.1.held = bf16[4,16,30080]{2,1,0:T(8,128)(2,1)S(1)} custom-call(bf16[64,30016]{1,0:T(8,128)(2,1)} %v_hbm.1, bf16[2,8,30016]{2,1,0:T(8,128)(2,1)} %r_hbm.1, f32[2,256,256]{2,1,0:T(8,128)} %f_hbm.1), custom_call_target="tpu_custom_call" | custom-call | tf_op jit(solution)/shard_map/back_transform/pallas_call | solution.py:510
  120.8 1.9 %joined.1 = bf16[16,120064]{1,0:T(8,128)(2,1)} custom-call(bf16[4,16,30080]{2,1,0:T(8,128)(2,1)S(1)} %back_transform.1.held), custom_call_target="tpu_custom_call" | custom-call | tf_op jit(solution)/shard_map/joined/pallas_call | solution.py:549

commit v10 on v9

--- a/solution.py
+++ b/solution.py
@@ -412,9 +412,9 @@
     second_half(range(AHEAD[1], PIECES))
     p_out(1)
     s_shared(0)
-    results(0, 0, 2)
+    results(0, 0, 1)
     s_out(1)
-    results(0, 2, 6)
+    results(0, 1, 6)
     s_shared(1)
     results(1, 0, 6)
 

time: 123 us -> 123 us (level)
  no operation moved by 1% of the time
where the time goes in v10:
time: 123 us
  Pallas kernels  123 us (100%)
    pallas_call x1, Pallas kernels, body(): pl.pallas_call(functools.partial(kernel, dims), out_shape=pltpu.VMEM((R,...  121 us

profile of v10, /device:TPU:1, one launch (start us, length us, event | category | flops | bytes accessed | tf_op | source)
XLA Modules:
  0.0 122.8 jit_solution(8755577736085030186)
XLA Ops:
  0.0 120.8 %back_transform.1.held = bf16[4,16,30080]{2,1,0:T(8,128)(2,1)S(1)} custom-call(bf16[64,30016]{1,0:T(8,128)(2,1)} %v_hbm.1, bf16[2,8,30016]{2,1,0:T(8,128)(2,1)} %r_hbm.1, f32[2,256,256]{2,1,0:T(8,128)} %f_hbm.1), custom_call_target="tpu_custom_call" | custom-call | tf_op jit(solution)/shard_map/back_transform/pallas_call | solution.py:510
  120.8 1.9 %joined.1 = bf16[16,120064]{1,0:T(8,128)(2,1)} custom-call(bf16[4,16,30080]{2,1,0:T(8,128)(2,1)S(1)} %back_transform.1.held), custom_call_target="tpu_custom_call" | custom-call | tf_op jit(solution)/shard_map/joined/pallas_call | solution.py:549
